TPU v7x, 256 devices: a whole 4x4x8 slice. The times are simulated.
256 devices in a mesh: ty: 8 (over y_hi, x), tx: 32 (over y_lo, z, core).
Axes of the slice: x: 4, y: 4 (y_hi: 2, y_lo: 2; y = y_hi * 2 + y_lo), z: 8, core: 2. Of those that a mesh axis runs over, the one named last changes fastest.
Arguments:
- state: float32 [3, 1024, 16384], P(None, 'ty', 'tx'), may hold values from -6 to 6
- cut_mask: int32 [1024, 16384], P('ty', 'tx'), may hold values from 0 to 1, as said below
- fraction: int32 [1024, 16384], P('ty', 'tx'), may hold values from 256 to 1024
- neighbourhood: int32 [1024, 16384], P('ty', 'tx'), may hold values from 16 to 511, as said below
- tile_flags: int32 [8, 128], P('ty', 'tx'), may hold values from 0 to 1, as said below
- centroid_offset: float32 [2, 1024, 16384], P(None, 'ty', 'tx'), may hold values from -0.45 to 0.45
Outputs:
- redistributed: float32 [3, 1024, 16384], P(None, 'ty', 'tx')
Inputs may be any that keep to these rules, and one draw needn't show every extreme that they name: Bit 3 (dy + 1) + (dx + 1) says whether the cell dy rows and dx columns away belongs to the cell's neighbourhood; bit 4 is always set, and no bit names a cell outside the grid. At the four corner cells of every block of 128 x 512 cells (rows k * 128 and k * 128 + 127, likewise for columns) every bit that names a cell inside the grid is set. `tile_flags`: the tiles at the four corners of every block of 128 x 512 cells are flagged. `cut_mask`: the four corner cells of every block of 128 x 512 cells are cut.
All inputs are finite; a program needn't handle non-finite values.
Results may differ from a plain program's by a relative error of at most 0.0003.
Values sent between devices are 32-bit elements; how exact they have to be, the bound alone decides.
No kernel may reach another device: no remote copies, remote signals or barrier semaphores. Data moves between devices by JAX's collectives and lax.ppermute only.
A program may use at most 64 MiB of HBM per device.

v0:
```python
import jax
import jax.numpy as jnp
from jax import lax
from jax.sharding import PartitionSpec as P

TILE = 128
STEPS = 1


courant = 0.1
cell_offsets = [(row_step, col_step) for row_step in (-1, 0, 1) for col_step in (-1, 0, 1)]


def with_halo(value, sides, width):
    for axis, dim in sides:
        devices, length = (lax.axis_size(axis), value.shape[dim])
        up = [(i, (i + 1) % devices) for i in range(devices - 1)]
        down = [(j, i) for i, j in up]
        last = lax.slice_in_dim(value, length - width, length, axis=dim)
        initial = lax.slice_in_dim(value, 0, width, axis=dim)
        before = lax.ppermute(last, axis, up)
        after = lax.ppermute(initial, axis, down)
        value = jnp.concatenate([before, value, after], axis=dim)
    return value


def window(padded, row_step, col_step):
    height = padded.shape[-2] - 2
    width = padded.shape[-1] - 2
    return padded[..., 1 + row_step : 1 + row_step + height, 1 + col_step : 1 + col_step + width]


def spread(values, row_step, col_step):
    widths = [(0, 0)] * (values.ndim - 2) + [
        (1 + row_step, 1 - row_step),
        (1 + col_step, 1 - col_step),
    ]
    return jnp.pad(values, widths)


def pad_cells(values):
    widths = [(0, 0)] * (values.ndim - 2) + [(1, 1), (1, 1)]
    return jnp.pad(values, widths)


def members_of(code_bits, active):
    result = []
    for bit_index in range(9):
        bit_value = jnp.right_shift(code_bits, bit_index) & 1
        centre_value = 1 if bit_index == 4 else 0
        result.append(jnp.where(active > 0, bit_value, centre_value).astype(jnp.float32))
    return result


def advance(padded, inv_volume):
    centre = window(padded, 0, 0)
    eastern = window(padded, 0, 1)
    western = window(padded, 0, -1)
    northern = window(padded, 1, 0)
    southern = window(padded, -1, 0)
    mass_flux = 0.5 * (eastern[1] - western[1] + (northern[2] - southern[2]))
    xmom_flux = 0.5 * (eastern[0] - western[0])
    ymom_flux = 0.5 * (northern[0] - southern[0])
    smoothing = eastern + western + northern + southern - 4.0 * centre
    divergence = jnp.stack([mass_flux, xmom_flux, ymom_flux]) - 0.5 * smoothing
    return centre - courant * inv_volume * divergence


def geometry_sums(members, share_pad, offset_pad):
    total = 0.0
    sum_x = 0.0
    sum_y = 0.0
    for bit_index, (row_step, col_step) in enumerate(cell_offsets):
        weight = members[bit_index] * window(share_pad, row_step, col_step)
        total = total + weight
        sum_x = sum_x + weight * (col_step + window(offset_pad[0], row_step, col_step))
        sum_y = sum_y + weight * (row_step + window(offset_pad[1], row_step, col_step))
    return (total, sum_x, sum_y)


def averages(members, share_pad, star_pad, total):
    summed = 0.0
    for bit_index, (row_step, col_step) in enumerate(cell_offsets):
        weight = members[bit_index] * window(share_pad, row_step, col_step)
        summed = summed + weight * window(star_pad, row_step, col_step)
    return summed / total


def slopes(average, average_pad, centroid, centroid_pad):
    moment_xx = 1.0
    moment_xy = 0.0
    moment_yy = 1.0
    right_x = 0.0
    right_y = 0.0
    for row_step, col_step in cell_offsets:
        if row_step == 0 and col_step == 0:
            continue
        apart_x = col_step + window(centroid_pad[0], row_step, col_step) - centroid[0]
        apart_y = row_step + window(centroid_pad[1], row_step, col_step) - centroid[1]
        change = window(average_pad, row_step, col_step) - average
        moment_xx = moment_xx + apart_x * apart_x
        moment_xy = moment_xy + apart_x * apart_y
        moment_yy = moment_yy + apart_y * apart_y
        right_x = right_x + apart_x * change
        right_y = right_y + apart_y * change
    determinant = moment_xx * moment_yy - moment_xy * moment_xy
    slope_x = (moment_yy * right_x - moment_xy * right_y) / determinant
    slope_y = (moment_xx * right_y - moment_xy * right_x) / determinant
    return (slope_x, slope_y)


def pushed(members, kappa_cell, average, slope_x, slope_y, centroid, offset_pad):
    extended = 0.0
    for bit_index, (row_step, col_step) in enumerate(cell_offsets):
        toward_x = col_step + window(offset_pad[0], row_step, col_step) - centroid[0]
        toward_y = row_step + window(offset_pad[1], row_step, col_step) - centroid[1]
        value = (
            members[bit_index] * kappa_cell * (average + slope_x * toward_x + slope_y * toward_y)
        )
        extended = extended + spread(value, row_step, col_step)
    return extended


def margin_solve(state, active, fraction, neighbourhood, offset_cell):
    depth = 4
    ones_cell = jnp.ones_like(offset_cell[0])
    static_stack = jnp.stack(
        [
            neighbourhood.astype(jnp.float32),
            active.astype(jnp.float32),
            fraction.astype(jnp.float32),
            offset_cell[0],
            offset_cell[1],
            ones_cell,
        ]
    )
    static_pad = with_halo(static_stack, (("ty", 1), ("tx", 2)), depth)
    inside = static_pad[5]
    inside_on = inside > 0.5
    active_wide = static_pad[1].astype(jnp.int32)
    code_wide = static_pad[0].astype(jnp.int32)
    members = [entry * inside for entry in members_of(code_wide, active_wide)]
    kappa_wide = jnp.where(
        inside_on, jnp.where(active_wide > 0, static_pad[2] * (1.0 / 1024.0), 1.0), 0.0
    )
    inv_volume = 1.0 / jnp.where(inside_on, kappa_wide, 1.0)
    offset_wide = static_pad[3:5]
    offset_pad = pad_cells(offset_wide)
    gathered = 0.0
    for bit_index, (row_step, col_step) in enumerate(cell_offsets):
        gathered = gathered + spread(members[bit_index] * kappa_wide, row_step, col_step)
    coverage_wide = gathered[1:-1, 1:-1]
    share_wide = jnp.where(inside_on, kappa_wide / jnp.where(inside_on, coverage_wide, 1.0), 0.0)
    share_pad = pad_cells(share_wide)
    total, sum_x, sum_y = geometry_sums(members, share_pad, offset_pad)
    total_safe = jnp.where(inside_on, total, 1.0)
    centroid = jnp.stack([sum_x / total_safe, sum_y / total_safe]) * inside
    centroid_pad = pad_cells(centroid)
    coverage_own = coverage_wide[depth:-depth, depth:-depth]

    def wide_step(step_index, current):
        current_pad = with_halo(current, (("ty", 1), ("tx", 2)), depth)
        star = advance(pad_cells(current_pad), inv_volume)
        average = averages(members, share_pad, pad_cells(star), total_safe) * inside
        slope_x, slope_y = slopes(average, pad_cells(average), centroid, centroid_pad)
        extended = pushed(members, kappa_wide, average, slope_x, slope_y, centroid, offset_pad)
        return extended[:, 1 + depth : -1 - depth, 1 + depth : -1 - depth] / coverage_own

    return lax.fori_loop(0, STEPS, wide_step, state)


def body(state, cut_mask, fraction, neighbourhood, tile_flags, centroid_offset):
    flag_rows, flag_cols = tile_flags.shape
    flag_cells = jnp.broadcast_to(
        tile_flags[:, None, :, None], (flag_rows, TILE, flag_cols, TILE)
    ).reshape(flag_rows * TILE, flag_cols * TILE)
    active = flag_cells * cut_mask
    offset_cell = centroid_offset * active.astype(jnp.float32)
    return margin_solve(state, active, fraction, neighbourhood, offset_cell)


def solution(mesh):
    placed = (
        P(None, "ty", "tx"),
        P("ty", "tx"),
        P("ty", "tx"),
        P("ty", "tx"),
        P("ty", "tx"),
        P(None, "ty", "tx"),
    )
    return jax.shard_map(
        body, mesh=mesh, in_specs=placed, out_specs=P(None, "ty", "tx"), check_vma=False
    )
```

profile of v0, /device:TPU:103, one launch (start us, length us, event | category | flops | bytes accessed | tf_op | source)
XLA Modules:
  0.0 96.2 jit_solution(17248962217263487266)
XLA Ops:
  0.0 0.9 fusion.92
  0.9 4.7 %collective-permute-start.4 = (f32[3,4,512]{2,1,0:T(4,128)S(1)}, f32[3,4,512]{2,1,0:T(4,128)S(1)}, u32[]{:S(2)}, u32[]{:S(2)}) collective-permute-start(f32[3,4,512]{2,1,0:T(4,128)S(1)} %get-tuple-element.159), channel_id=1, source_target_pairs={{0,32},{32,64},{64,96},{96,128},{128,160},{160,192},{192,224},{1,3... | collective-permute-start | bytes 73736 | tf_op jit(solution)/shard_map/while/body/eval_jaxpr/ppermute | solution.py:21
  5.7 1.9 %collective-permute-start.5 = (f32[3,4,512]{2,1,0:T(4,128)S(1)}, f32[3,4,512]{2,1,0:T(4,128)S(1)}, u32[]{:S(2)}, u32[]{:S(2)}) collective-permute-start(f32[3,4,512]{2,1,0:T(4,128)S(1)} %get-tuple-element.160), channel_id=1, source_target_pairs={{32,0},{64,32},{96,64},{128,96},{160,128},{192,160},{224,192},{33,... | collective-permute-start | bytes 73736 | tf_op jit(solution)/shard_map/while/body/eval_jaxpr/ppermute | solution.py:22
  7.6 1.0 %bitcast_dynamic-update-slice_fusion.2 = f32[6,128,512]{2,1,0:T(8,128)S(1)} fusion(s32[128,512]{1,0:T(8,128)} %param.9), kind=kLoop, calls=%fused_computation.216 | loop fusion | flops 65535 | bytes 524288
  8.6 0.1 broadcast_bitcast_fusion
  8.7 1.0 %bitcast_dynamic-update-slice_fusion.1 = (f32[6,128,512]{2,1,0:T(8,128)S(1)}, f32[128,512]{1,0:T(8,128)S(1)}) fusion(f32[6,128,512]{2,1,0:T(8,128)S(1)} %bitcast_dynamic-update-slice_fusion.2, s32[128,512]{1,0:T(8,128)} %param.7, s32[512]{0:T(512)S(1)} %broadcast_bitcast_fusion), kind=kLoop, calls=%fused_computation.215 | loop fusion | flops 131072 | bytes 788480
  9.8 0.1 multiply_dynamic-update-slice_fusion
  9.9 4.0 %collective-permute-done.5 = f32[3,4,512]{2,1,0:T(4,128)S(1)} collective-permute-done((f32[3,4,512]{2,1,0:T(4,128)S(1)}, f32[3,4,512]{2,1,0:T(4,128)S(1)}, u32[]{:S(2)}, u32[]{:S(2)}) %collective-permute-start.5) | collective-permute-done | bytes 24608 | tf_op jit(solution)/shard_map/while/body/eval_jaxpr/ppermute | solution.py:22
  13.9 0.1 pad_maximum_fusion.7
  14.0 6.7 %collective-permute-start.6 = (f32[3,136,4]{2,1,0:T(8,128)S(1)}, f32[3,136,4]{2,1,0:T(8,128)S(1)}, u32[]{:S(2)}, u32[]{:S(2)}) collective-permute-start(f32[3,136,4]{2,1,0:T(8,128)S(1)} %get-tuple-element.157), channel_id=1, source_target_pairs={{0,1},{1,2},{2,3},{3,4},{4,5},{5,6},{6,7},{7,8},{8,9},{9,10},{10,1... | collective-permute-start | bytes 19592 | tf_op jit(solution)/shard_map/while/body/eval_jaxpr/ppermute | solution.py:21
  20.8 1.9 %collective-permute-start.7 = (f32[3,136,4]{2,1,0:T(8,128)S(1)}, f32[3,136,4]{2,1,0:T(8,128)S(1)}, u32[]{:S(2)}, u32[]{:S(2)}) collective-permute-start(f32[3,136,4]{2,1,0:T(8,128)S(1)} %get-tuple-element.158), channel_id=1, source_target_pairs={{1,0},{2,1},{3,2},{4,3},{5,4},{6,5},{7,6},{8,7},{9,8},{10,9},{11,1... | collective-permute-start | bytes 19592 | tf_op jit(solution)/shard_map/while/body/eval_jaxpr/ppermute | solution.py:22
  22.7 2.1 %collective-permute-start = (f32[6,4,512]{2,1,0:T(4,128)S(1)}, f32[6,4,512]{2,1,0:T(4,128)S(1)}, u32[]{:S(2)}, u32[]{:S(2)}) collective-permute-start(f32[6,4,512]{2,1,0:T(4,128)S(1)} %get-tuple-element.115), channel_id=1, source_target_pairs={{0,32},{32,64},{64,96},{96,128},{128,160},{160,192},{192,224},{1,3... | collective-permute-start | bytes 147464 | tf_op jit(solution)/shard_map/ppermute | solution.py:21
  24.9 3.1 %collective-permute-start.1 = (f32[6,4,512]{2,1,0:T(4,128)S(1)}, f32[6,4,512]{2,1,0:T(4,128)S(1)}, u32[]{:S(2)}, u32[]{:S(2)}) collective-permute-start(f32[6,4,512]{2,1,0:T(4,128)S(1)} %get-tuple-element.116), channel_id=1, source_target_pairs={{32,0},{64,32},{96,64},{128,96},{160,128},{192,160},{224,192},{33,... | collective-permute-start | bytes 147464 | tf_op jit(solution)/shard_map/ppermute | solution.py:22
  28.0 1.1 %collective-permute-done.7 = f32[3,136,4]{2,1,0:T(8,128)S(1)} collective-permute-done((f32[3,136,4]{2,1,0:T(8,128)S(1)}, f32[3,136,4]{2,1,0:T(8,128)S(1)}, u32[]{:S(2)}, u32[]{:S(2)}) %collective-permute-start.7) | collective-permute-done | bytes 6560 | tf_op jit(solution)/shard_map/while/body/eval_jaxpr/ppermute | solution.py:22
  29.1 0.4 pad_maximum_fusion
  29.5 4.1 %collective-permute-done.1 = f32[6,4,512]{2,1,0:T(4,128)S(1)} collective-permute-done((f32[6,4,512]{2,1,0:T(4,128)S(1)}, f32[6,4,512]{2,1,0:T(4,128)S(1)}, u32[]{:S(2)}, u32[]{:S(2)}) %collective-permute-start.1) | collective-permute-done | bytes 49184 | tf_op jit(solution)/shard_map/ppermute | solution.py:22
  33.6 0.2 pad_maximum_fusion.3
  33.8 6.0 %collective-permute-start.2 = (f32[6,136,4]{2,1,0:T(8,128)S(1)}, f32[6,136,4]{2,1,0:T(8,128)S(1)}, u32[]{:S(2)}, u32[]{:S(2)}) collective-permute-start(f32[6,136,4]{2,1,0:T(8,128)S(1)} %get-tuple-element.113), channel_id=1, source_target_pairs={{0,1},{1,2},{2,3},{3,4},{4,5},{5,6},{6,7},{7,8},{8,9},{9,10},{10,1... | collective-permute-start | bytes 39176 | tf_op jit(solution)/shard_map/ppermute | solution.py:21
  39.8 1.9 %collective-permute-start.3 = (f32[6,136,4]{2,1,0:T(8,128)S(1)}, f32[6,136,4]{2,1,0:T(8,128)S(1)}, u32[]{:S(2)}, u32[]{:S(2)}) collective-permute-start(f32[6,136,4]{2,1,0:T(8,128)S(1)} %get-tuple-element.114), channel_id=1, source_target_pairs={{1,0},{2,1},{3,2},{4,3},{5,4},{6,5},{7,6},{8,7},{9,8},{10,9},{11,1... | collective-permute-start | bytes 39176 | tf_op jit(solution)/shard_map/ppermute | solution.py:22
  41.7 0.4 fusion.16
  42.2 2.6 %collective-permute-done.2 = f32[6,136,4]{2,1,0:T(8,128)S(1)} collective-permute-done((f32[6,136,4]{2,1,0:T(8,128)S(1)}, f32[6,136,4]{2,1,0:T(8,128)S(1)}, u32[]{:S(2)}, u32[]{:S(2)}) %collective-permute-start.2) | collective-permute-done | bytes 13088 | tf_op jit(solution)/shard_map/ppermute | solution.py:21
  44.8 5.6 %collective-permute-done.3 = f32[6,136,4]{2,1,0:T(8,128)S(1)} collective-permute-done((f32[6,136,4]{2,1,0:T(8,128)S(1)}, f32[6,136,4]{2,1,0:T(8,128)S(1)}, u32[]{:S(2)}, u32[]{:S(2)}) %collective-permute-start.3) | collective-permute-done | bytes 13088 | tf_op jit(solution)/shard_map/ppermute | solution.py:22
  50.4 1.3 %multiply_bitcast_fusion.1 = (f32[136,520]{1,0:T(8,128)}, f32[1,136,520]{2,1,0:T(8,128)S(1)}, f32[1,136,520]{2,1,0:T(8,128)S(1)}, s32[1,136,520]{2,1,0:T(8,128)S(1)}, pred[1,136,520]{2,1,0:T(8,128)(4,1)S(1)}) fusion(f32[6,136,4]{2,1,0:T(8,128)S(1)} %collective-permute-done.3, f32[6,4,512]{2,1,0:T(4,128)S(1)} %collective-permute-done.1, ...), kind=kLoop, calls=%fused_computation.194 | loop fusion | flops 2050880 | bytes 2899520 | tf_op jit(solution)/shard_map/while/body/eval_jaxpr/mul | solution.py:118
  51.7 2.0 %fusion.53 = (f32[136,520]{1,0:T(8,128)}, f32[136,520]{1,0:T(8,128)}, f32[136,520]{1,0:T(8,128)}, f32[136,520]{1,0:T(8,128)}, f32[136,520]{1,0:T(8,128)}, /*inde...) fusion(f32[1,136,520]{2,1,0:T(8,128)S(1)} %get-tuple-element.48, ...), kind=kLoop, calls=%fused_computation.168 | loop fusion | flops 3748160 | bytes 3465280 | tf_op jit(solution)/shard_map/while/body/eval_jaxpr/mul | solution.py:118
  53.7 0.6 fusion.66
  54.4 0.7 pad_add_fusion.7
  55.0 0.2 fusion.35
  55.2 1.2 %add_select_fusion = (f32[136,520]{1,0:T(8,128)S(1)}, f32[136,520]{1,0:T(8,128)S(1)}, f32[136,520]{1,0:T(8,128)S(1)}, f32[136,520]{1,0:T(8,128)S(1)}, f32[136,52...) fusion(f32[1,136,520]{2,1,0:T(8,128)S(1)} %get-tuple-element.48, ...), kind=kLoop, calls=%fused_computation.175 | loop fusion | flops 4808960 | bytes 4313920 | tf_op jit(solution)/shard_map/jit(_where)/select_n | solution.py:156
  56.4 0.4 select_maximum_fusion
  56.9 0.1 slice_bitcast_fusion.1
  56.9 0.7 divide_bitcast_fusion.1
  57.7 0.8 divide_bitcast_fusion
  58.4 0.1 maximum_multiply_fusion
  58.5 0.3 fusion.13
  58.8 2.2 %slice_subtract_fusion.17 = (f32[136,520]{1,0:T(8,128)}, f32[136,520]{1,0:T(8,128)}, f32[136,520]{1,0:T(8,128)}, f32[136,520]{1,0:T(8,128)}, f32[136,520]{1,0:T(...) fusion(f32[138,522]{1,0:T(8,128)S(1)} %get-tuple-element.161, ...), kind=kLoop, calls=%fused_computation.201 | loop fusion | flops 1060800 | bytes 5374720 | tf_op jit(solution)/shard_map/while/body/eval_jaxpr/sub | solution.py:115
  61.0 2.3 %fusion.61 = (f32[136,520]{1,0:T(8,128)}, f32[136,520]{1,0:T(8,128)}, f32[136,520]{1,0:T(8,128)}, f32[136,520]{1,0:T(8,128)}, f32[136,520]{1,0:T(8,128)}, /*inde...) fusion(f32[138,522]{1,0:T(8,128)S(1)} %get-tuple-element.162, ...), kind=kLoop, calls=%fused_computation.209 | loop fusion | flops 1060800 | bytes 5374720 | tf_op jit(solution)/shard_map/while/body/eval_jaxpr/sub | solution.py:116
  63.2 0.9 slice.616
  64.1 0.7 fusion.1
  64.8 1.9 %divide_multiply_fusion = f32[3,136,520]{2,1,0:T(8,128)S(1)} fusion(f32[3,136,520]{2,1,0:T(8,128)S(1)} %fusion.1, f32[136,520]{1,0:T(8,128)S(1)} %bitcast.276, f32[136,520]{1,0:T(8,128)S(1)} %get-tuple-element.93, f32[136,520]{1,0:T(8,128)S(1)} %get-tuple-element.102, f32[136,520]{1,0:T(8,128)S(1)} %get-tuple-element.101, ...), kind=kLoop, calls=%fused_computation.30 | loop fusion | flops 4031040 | bytes 4808960 | tf_op jit(solution)/shard_map/while/body/eval_jaxpr/mul | solution.py:164
  66.8 2.5 %multiply_subtract_fusion = (f32[136,520]{1,0:T(8,128)}, f32[136,520]{1,0:T(8,128)}, f32[136,520]{1,0:T(8,128)}, f32[136,520]{1,0:T(8,128)}, f32[136,520]{1,0:T(...) fusion(f32[2,136,520]{2,1,0:T(8,128)S(1)} %maximum_multiply_fus, ...), kind=kLoop, calls=%fused_computation.169 | loop fusion | flops 5516160 | bytes 10749440 | tf_op jit(solution)/shard_map/while/body/eval_jaxpr/sub | solution.py:106
  69.2 4.9 %multiply_add_fusion.1 = (f32[3,136,520]{2,1,0:T(8,128)}, f32[3,136,520]{2,1,0:T(8,128)}) fusion(f32[136,520]{1,0:T(8,128)S(1)} %get-tuple-element.92, f32[136,520]{1,0:T(8,128)S(1)} %get-tuple-element.91, f32[136,520]{1,0:T(8,128)S(1)} %get-tuple-element.90, f32[136,520]{1,0:T(8,128)S(1)} %get-tuple-element.89, f32[136,520]{1,0:T(8,128)S(1)} %get-tuple-element.88, ...), kind=kLoop, calls=%fused_computation.21 | loop fusion | flops 9759360 | bytes 7072000 | tf_op jit(solution)/shard_map/while/body/eval_jaxpr/add | solution.py:104
  74.1 5.7 %add_multiply_fusion.8 = (f32[3,136,520]{2,1,0:T(8,128)}, f32[3,136,520]{2,1,0:T(8,128)}, f32[3,136,520]{2,1,0:T(8,128)}) fusion(f32[136,520]{1,0:T(8,128)} %get-tuple-element.151, f32[136,520]{1,0:T(8,128)} %get-tuple-element.142, f32[136,520]{1,0:T(8,128)} %get-tuple-element.46, f32[136,520]{1,0:T(8,128)} %get-tuple-element.51, ...), kind=kLoop, calls=%fused_computation.17 | loop fusion | flops 6789120 | bytes 10183680 | tf_op jit(solution)/shard_map/while/body/eval_jaxpr/mul | solution.py:118
  79.9 5.9 %add_multiply_fusion.6 = (f32[3,136,520]{2,1,0:T(8,128)}, f32[3,136,520]{2,1,0:T(8,128)}, f32[3,136,520]{2,1,0:T(8,128)}) fusion(f32[3,136,520]{2,1,0:T(8,128)} %get-tuple-element.45, f32[3,136,520]{2,1,0:T(8,128)} %get-tuple-element.44, f32[136,520]{1,0:T(8,128)} %get-tuple-element.150, f32[136,520]{1,0:T(8,128)} %get-tuple-element.141, ...), kind=kLoop, calls=%fused_computation.15 | loop fusion | flops 7213440 | bytes 10749440 | tf_op jit(solution)/shard_map/while/body/eval_jaxpr/mul | solution.py:118
  85.8 5.9 %add_multiply_fusion.7 = (f32[3,136,520]{2,1,0:T(8,128)S(1)}, f32[3,136,520]{2,1,0:T(8,128)S(1)}, f32[3,136,520]{2,1,0:T(8,128)S(1)}, f32[3,136,520]{2,1,0:T(8,128)S(1)}, f32[3,136,520]{2,1,0:T(8,128)S(1)}) fusion(f32[3,136,520]{2,1,0:T(8,128)} %get-tuple-element.45, f32[3,136,520]{2,1,0:T(8,128)} %get-tuple-element.44, f32[136,520]{1,0:T(8,128)} %get-tuple-element.143, ...), kind=kLoop, calls=%fused_computation.16 | loop fusion | flops 9335040 | bytes 14144000 | tf_op jit(solution)/shard_map/while/body/eval_jaxpr/mul | solution.py:118
  91.8 0.6 pad_add_fusion
  92.4 0.6 copy-done.6
  93.0 0.3 copy-done.7
  93.3 2.9 %fusion.8 = f32[3,128,512]{2,1,0:T(8,128)} fusion(f32[3,136,520]{2,1,0:T(8,128)S(1)} %copy-done.7, f32[3,136,520]{2,1,0:T(8,128)S(1)} %get-tuple-element.106, f32[3,136,520]{2,1,0:T(8,128)S(1)} %get-tuple-element.107, f32[3,136,520]{2,1,0:T(8,128)S(1)} %get-tuple-element.108, f32[3,136,520]{2,1,0:T(8,128)S(1)} %get-tuple-element.109, ...), kind=kLoop, calls=%fused_computation.51 | loop fusion | flops 1376256 | bytes 6926848 | tf_op jit(solution)/shard_map/while/body/eval_jaxpr/div | solution.py:167
  (30 shorter events, 0.2 us)
Async XLA Ops:
  0.0 8.6 %copy-start = (s32[1,4]{1,0:T(1,128)S(1)}, s32[1,4]{1,0:T(1,128)}, u32[]{:S(2)}) copy-start(s32[1,4]{1,0:T(1,128)} %param.10) | copy-start | bytes 52
  0.0 9.7 %copy-start.12 = (s32[128,512]{1,0:T(8,128)S(1)}, s32[128,512]{1,0:T(8,128)}, u32[]{:S(2)}) copy-start(s32[128,512]{1,0:T(8,128)} %param.8) | copy-start | bytes 786436
  0.0 9.8 %copy-start.11 = (f32[2,128,512]{2,1,0:T(8,128)S(1)}, f32[2,128,512]{2,1,0:T(8,128)}, u32[]{:S(2)}) copy-start(f32[2,128,512]{2,1,0:T(8,128)} %param.11) | copy-start | bytes 1572868
  0.9 8.9 %collective-permute-start.4 = (f32[3,4,512]{2,1,0:T(4,128)S(1)}, f32[3,4,512]{2,1,0:T(4,128)S(1)}, u32[]{:S(2)}, u32[]{:S(2)}) collective-permute-start(f32[3,4,512]{2,1,0:T(4,128)S(1)} %get-tuple-element.159), channel_id=1, source_target_pairs={{0,32},{32,64},{64,96},{96,128},{128,160},{160,192},{192,224},{1,3... | collective-permute-start | bytes 73736 | tf_op jit(solution)/shard_map/while/body/eval_jaxpr/ppermute | solution.py:21
  5.7 8.2 %collective-permute-start.5 = (f32[3,4,512]{2,1,0:T(4,128)S(1)}, f32[3,4,512]{2,1,0:T(4,128)S(1)}, u32[]{:S(2)}, u32[]{:S(2)}) collective-permute-start(f32[3,4,512]{2,1,0:T(4,128)S(1)} %get-tuple-element.160), channel_id=1, source_target_pairs={{32,0},{64,32},{96,64},{128,96},{160,128},{192,160},{224,192},{33,... | collective-permute-start | bytes 73736 | tf_op jit(solution)/shard_map/while/body/eval_jaxpr/ppermute | solution.py:22
  8.6 5.3 %copy-start.9 = (f32[3,128,512]{2,1,0:T(8,128)S(1)}, f32[3,128,512]{2,1,0:T(8,128)}, u32[]{:S(2)}) copy-start(f32[3,128,512]{2,1,0:T(8,128)} %param.6) | copy-start | bytes 2359300
  14.0 14.0 %collective-permute-start.6 = (f32[3,136,4]{2,1,0:T(8,128)S(1)}, f32[3,136,4]{2,1,0:T(8,128)S(1)}, u32[]{:S(2)}, u32[]{:S(2)}) collective-permute-start(f32[3,136,4]{2,1,0:T(8,128)S(1)} %get-tuple-element.157), channel_id=1, source_target_pairs={{0,1},{1,2},{2,3},{3,4},{4,5},{5,6},{6,7},{7,8},{8,9},{9,10},{10,1... | collective-permute-start | bytes 19592 | tf_op jit(solution)/shard_map/while/body/eval_jaxpr/ppermute | solution.py:21
  20.8 8.3 %collective-permute-start.7 = (f32[3,136,4]{2,1,0:T(8,128)S(1)}, f32[3,136,4]{2,1,0:T(8,128)S(1)}, u32[]{:S(2)}, u32[]{:S(2)}) collective-permute-start(f32[3,136,4]{2,1,0:T(8,128)S(1)} %get-tuple-element.158), channel_id=1, source_target_pairs={{1,0},{2,1},{3,2},{4,3},{5,4},{6,5},{7,6},{8,7},{9,8},{10,9},{11,1... | collective-permute-start | bytes 19592 | tf_op jit(solution)/shard_map/while/body/eval_jaxpr/ppermute | solution.py:22
  22.7 6.8 %collective-permute-start = (f32[6,4,512]{2,1,0:T(4,128)S(1)}, f32[6,4,512]{2,1,0:T(4,128)S(1)}, u32[]{:S(2)}, u32[]{:S(2)}) collective-permute-start(f32[6,4,512]{2,1,0:T(4,128)S(1)} %get-tuple-element.115), channel_id=1, source_target_pairs={{0,32},{32,64},{64,96},{96,128},{128,160},{160,192},{192,224},{1,3... | collective-permute-start | bytes 147464 | tf_op jit(solution)/shard_map/ppermute | solution.py:21
  24.9 8.7 %collective-permute-start.1 = (f32[6,4,512]{2,1,0:T(4,128)S(1)}, f32[6,4,512]{2,1,0:T(4,128)S(1)}, u32[]{:S(2)}, u32[]{:S(2)}) collective-permute-start(f32[6,4,512]{2,1,0:T(4,128)S(1)} %get-tuple-element.116), channel_id=1, source_target_pairs={{32,0},{64,32},{96,64},{128,96},{160,128},{192,160},{224,192},{33,... | collective-permute-start | bytes 147464 | tf_op jit(solution)/shard_map/ppermute | solution.py:22
  33.8 11.0 %collective-permute-start.2 = (f32[6,136,4]{2,1,0:T(8,128)S(1)}, f32[6,136,4]{2,1,0:T(8,128)S(1)}, u32[]{:S(2)}, u32[]{:S(2)}) collective-permute-start(f32[6,136,4]{2,1,0:T(8,128)S(1)} %get-tuple-element.113), channel_id=1, source_target_pairs={{0,1},{1,2},{2,3},{3,4},{4,5},{5,6},{6,7},{7,8},{8,9},{9,10},{10,1... | collective-permute-start | bytes 39176 | tf_op jit(solution)/shard_map/ppermute | solution.py:21
  39.8 10.6 %collective-permute-start.3 = (f32[6,136,4]{2,1,0:T(8,128)S(1)}, f32[6,136,4]{2,1,0:T(8,128)S(1)}, u32[]{:S(2)}, u32[]{:S(2)}) collective-permute-start(f32[6,136,4]{2,1,0:T(8,128)S(1)} %get-tuple-element.114), channel_id=1, source_target_pairs={{1,0},{2,1},{3,2},{4,3},{5,4},{6,5},{7,6},{8,7},{9,8},{10,9},{11,1... | collective-permute-start | bytes 39176 | tf_op jit(solution)/shard_map/ppermute | solution.py:22
  56.4 8.4 %copy-start.1 = (f32[136,520]{1,0:T(8,128)}, f32[136,520]{1,0:T(8,128)S(1)}, u32[]{:S(2)}) copy-start(f32[136,520]{1,0:T(8,128)S(1)} %get-tuple-element.100) | copy-start | bytes 848644
  56.4 8.4 %copy-start.2 = (f32[136,520]{1,0:T(8,128)}, f32[136,520]{1,0:T(8,128)S(1)}, u32[]{:S(2)}) copy-start(f32[136,520]{1,0:T(8,128)S(1)} %get-tuple-element.101) | copy-start | bytes 848644
  56.4 8.4 %copy-start.3 = (f32[136,520]{1,0:T(8,128)}, f32[136,520]{1,0:T(8,128)S(1)}, u32[]{:S(2)}) copy-start(f32[136,520]{1,0:T(8,128)S(1)} %get-tuple-element.102) | copy-start | bytes 848644
  56.4 8.4 %copy-start.4 = (f32[136,520]{1,0:T(8,128)}, f32[136,520]{1,0:T(8,128)S(1)}, u32[]{:S(2)}) copy-start(f32[136,520]{1,0:T(8,128)S(1)} %get-tuple-element.93) | copy-start | bytes 848644
  85.8 5.9 %copy-start.5 = (f32[3,136,520]{2,1,0:T(8,128)S(1)}, f32[3,136,520]{2,1,0:T(8,128)}, u32[]{:S(2)}) copy-start(f32[3,136,520]{2,1,0:T(8,128)} %get-tuple-element.43) | copy-start | bytes 2545924
  85.8 5.9 %copy-start.8 = (f32[3,136,520]{2,1,0:T(8,128)S(1)}, f32[3,136,520]{2,1,0:T(8,128)}, u32[]{:S(2)}) copy-start(f32[3,136,520]{2,1,0:T(8,128)} %get-tuple-element.110) | copy-start | bytes 2545924
  91.7 1.2 %copy-start.6 = (f32[3,136,520]{2,1,0:T(8,128)S(1)}, f32[3,136,520]{2,1,0:T(8,128)}, u32[]{:S(2)}) copy-start(f32[3,136,520]{2,1,0:T(8,128)} %get-tuple-element.111) | copy-start | bytes 2545924
  91.8 1.5 %copy-start.7 = (f32[3,136,520]{2,1,0:T(8,128)S(1)}, f32[3,136,520]{2,1,0:T(8,128)}, u32[]{:S(2)}) copy-start(f32[3,136,520]{2,1,0:T(8,128)} %get-tuple-element.112) | copy-start | bytes 2545924
  91.8 1.6 %copy-start.10 = (f32[128,512]{1,0:T(8,128)S(1)}, f32[128,512]{1,0:T(8,128)}, u32[]{:S(2)}) copy-start(f32[128,512]{1,0:T(8,128)} %slice.616) | copy-start | bytes 786436
where the time goes:
time: 96.6 us; the launch traced here: 96.2 us
  other arithmetic  46.9 us (49%)
  starting transfers between devices  28.5 us (30%)
  waiting for transfers between devices  17.3 us (18%)
  local copies, waits for them, and re-layouts  3.15 us (3%)
    mul x6, other arithmetic, pushed(): members[bit_index] * kappa_cell  21.5 us
    ppermute x4, starting transfers between devices, with_halo(): before = lax.ppermute(last, axis, up)  19.6 us
    ppermute x4, waiting for transfers between devices, with_halo(): after = lax.ppermute(initial, axis, down)  14.7 us
    ppermute x4, starting transfers between devices, with_halo(): after = lax.ppermute(initial, axis, down)  8.91 us
    add x1, other arithmetic, slopes(): right_x = right_x + apart_x * change  4.9 us
    div x1, other arithmetic, wide_step(): extended[:, 1 + depth:-1 - depth, 1 + depth:-1 - depth] / coverage_own  2.91 us
    ppermute x4, waiting for transfers between devices, with_halo(): before = lax.ppermute(last, axis, up)  2.6 us
    sub x1, other arithmetic, slopes(): determinant = moment_xx * moment_yy - moment_xy * moment_xy  2.49 us
  transfers between devices with their start and end apart: 8, of which 5 were waited for; matrix products, arithmetic and copies ran while one was open for 3% of the time, Pallas kernels for 0%

commit v1 on v0

v1 whole, which is shorter than its diff:
```python
import functools

import jax
import jax.numpy as jnp
from jax import lax
from jax.experimental import pallas as pl
from jax.experimental.pallas import tpu as pltpu
from jax.sharding import PartitionSpec as P

DEPTH = 4
LANES = 128
FIELDS = 7
PACKED = 4 * FIELDS
VMEM_LIMIT = 56 * 1024 * 1024

courant = 0.1


def paired(value, axis, other, first):
    length, width = lax.axis_size(axis), lax.axis_size(other)
    pairs = []
    for i in range(length):
        for j in range(width):
            mate = (i + 1 if (i - first) % 2 == 0 else i - 1, j)
            if not 0 <= mate[0] < length:
                mate = (i, j ^ 1)
            here = i * width + j
            there = mate[0] * width + mate[1]
            pairs.append((here, there))
    if axis == "tx":
        swap = lambda k: (k % width) * length + k // width
        pairs = [(swap(a), swap(b)) for a, b in pairs]
    return lax.ppermute(value, ("ty", "tx"), sorted(pairs))


def lane_index():
    return lax.broadcasted_iota(jnp.int32, (8, LANES), 1)


def from_west(values, west, lane):
    return [
        pltpu.roll(jnp.where(lane == LANES - 1, values[west[t]], values[t]), 1, 1)
        for t in range(len(values))
    ]


def from_east(values, east, lane):
    return [
        pltpu.roll(jnp.where(lane == 0, values[east[t]], values[t]), LANES - 1, 1)
        for t in range(len(values))
    ]


def inverse(value):
    guess = pl.reciprocal(value, approx=True)
    return guess * (2.0 - value * guess)


def store_members(mk, code, kappa, t, rows, order):
    for b in range(9):
        held = (code & (1 << order[b])) != 0
        mk[b, t, rows, :] = jnp.where(held, kappa, 0.0)


plain_order = (0, 1, 2, 3, 4, 5, 6, 7, 8)
swapped_order = (0, 3, 6, 1, 4, 7, 2, 5, 8)


class Fields:
    def __init__(self, mk, raw, rc, gath, cent, horiz, push):
        self.mk, self.raw, self.rc = mk, raw, rc
        self.gath, self.cent, self.horiz, self.push = gath, cent, horiz, push

    @staticmethod
    def shapes(tiles, rows):
        shape = lambda n: pltpu.VMEM((n, tiles, rows, LANES), jnp.float32)
        return [shape(9), shape(6), shape(1), shape(18), shape(5), shape(14), shape(9)]


def at(ref, i, t, base, step=0):
    return ref[i, t, pl.ds(base + step, 8), :]


def stage_share(s, tiles, west, east, base):
    lane = lane_index()
    n = len(tiles)
    sums = []
    for dx in (-1, 0, 1):
        group = []
        for t in tiles:
            total = at(s.mk, 4 + dx, t, base)
            total = total + at(s.mk, 1 + dx, t, base, 1)
            total = total + at(s.mk, 7 + dx, t, base, -1)
            group.append(total)
        sums.append(group)
    low = from_east(sums[0], east, lane)
    high = from_west(sums[2], west, lane)
    centre = [[at(s.raw, 3 + f, t, base) for t in tiles] for f in range(3)]
    easts = [from_east(c, east, lane) for c in centre]
    wests = [from_west(c, west, lane) for c in centre]
    outs = [[] for _ in range(6)]
    for k, t in enumerate(tiles):
        coverage = jnp.maximum(sums[1][k] + low[k] + high[k], 0.125)
        rc = inverse(coverage)
        s.rc[0, t, pl.ds(base, 8), :] = rc
        share = at(s.raw, 0, t, base) * rc
        rate = (0.5 * courant) * rc
        keep = share - 4.0 * rate
        c = [centre[f][k] for f in range(3)]
        e = [easts[f][k] for f in range(3)]
        w = [wests[f][k] for f in range(3)]
        north = [at(s.raw, 3 + f, t, base, 1) for f in range(3)]
        south = [at(s.raw, 3 + f, t, base, -1) for f in range(3)]
        flux = [(e[1] - w[1]) + (north[2] - south[2]), e[0] - w[0], north[0] - south[0]]
        outs[0].append(share)
        outs[1].append(share * at(s.raw, 1, t, base))
        outs[2].append(share * at(s.raw, 2, t, base))
        for f in range(3):
            around = (e[f] + w[f]) + (north[f] + south[f])
            outs[3 + f].append(keep * c[f] - rate * (flux[f] - around))
    for f in range(6):
        w = from_west(outs[f], west, lane)
        e = from_east(outs[f], east, lane)
        for k, t in enumerate(tiles):
            s.gath[3 * f, t, pl.ds(base, 8), :] = w[k]
            s.gath[3 * f + 1, t, pl.ds(base, 8), :] = outs[f][k]
            s.gath[3 * f + 2, t, pl.ds(base, 8), :] = e[k]


def stage_average(s, tiles, west, east, base):
    lane = lane_index()
    results = [[] for _ in range(5)]
    for t in tiles:
        weight = {}
        for dy in (-1, 0, 1):
            for dx in (-1, 0, 1):
                member = at(s.mk, 3 * (dy + 1) + dx + 1, t, base)
                weight[dy, dx] = (member, member * at(s.gath, 1 + dx, t, base, dy))
        cols = [weight[-1, d][1] + weight[0, d][1] + weight[1, d][1] for d in (-1, 0, 1)]
        total = cols[0] + cols[1] + cols[2]
        upper = weight[1, -1][1] + weight[1, 0][1] + weight[1, 1][1]
        lower = weight[-1, -1][1] + weight[-1, 0][1] + weight[-1, 1][1]
        sums = [cols[2] - cols[0], upper - lower, None, None, None]
        for f in range(5):
            for dy in (-1, 0, 1):
                for dx in (-1, 0, 1):
                    term = weight[dy, dx][0] * at(s.gath, 3 * (f + 1) + 1 + dx, t, base, dy)
                    sums[f] = term if sums[f] is None else sums[f] + term
        inv = inverse(jnp.maximum(total, 1e-3))
        for f in range(5):
            value = sums[f] * inv
            s.cent[f, t, pl.ds(base, 8), :] = value
            results[f].append(value)
    w = [from_west(r, west, lane) for r in results]
    e = [from_east(r, east, lane) for r in results]
    for k, t in enumerate(tiles):
        x = [w[0][k] - 1.0, results[0][k], e[0][k] + 1.0]
        v = [w[1][k], results[1][k], e[1][k]]
        a = [[w[2 + f][k], results[2 + f][k], e[2 + f][k]] for f in range(3)]
        add3 = lambda p: p[0] + p[1] + p[2]
        dot3 = lambda p, q: p[0] * q[0] + p[1] * q[1] + p[2] * q[2]
        made = [add3(x), add3(v), dot3(x, x), dot3(x, v), dot3(v, v)]
        made += [add3(a[f]) for f in range(3)]
        made += [dot3(x, a[f]) for f in range(3)]
        made += [dot3(v, a[f]) for f in range(3)]
        for i, value in enumerate(made):
            s.horiz[i, t, pl.ds(base, 8), :] = value


def stage_slope(s, tiles, base):
    for t in tiles:
        rows = lambda i: [at(s.horiz, i, t, base, d) for d in (-1, 0, 1)]
        add3 = lambda p: p[0] + p[1] + p[2]
        u, v = at(s.cent, 0, t, base), at(s.cent, 1, t, base)
        hx, hv = rows(0), rows(1)
        sum_x, sum_y = add3(hx), add3(hv)
        sum_xx = add3(rows(2)) + 1.0
        sum_xy = add3(rows(3)) + (hx[2] - hx[0])
        sum_yy = add3(rows(4)) + (2.0 * (hv[2] - hv[0]) + 7.0)
        mean_x = sum_x - 9.0 * u
        mean_y = sum_y - 9.0 * v
        moment_xx = sum_xx - u * (sum_x + mean_x)
        moment_yy = sum_yy - v * (sum_y + mean_y)
        moment_xy = sum_xy - u * sum_y - v * mean_x
        inv = inverse(moment_xx * moment_yy - moment_xy * moment_xy)
        moment_xx = moment_xx * inv
        moment_yy = moment_yy * inv
        moment_xy = moment_xy * inv
        for f in range(3):
            average = at(s.cent, 2 + f, t, base)
            ha = rows(5 + f)
            sum_a = add3(ha)
            right_x = add3(rows(8 + f)) - u * sum_a - average * mean_x
            right_y = add3(rows(11 + f)) + (ha[2] - ha[0]) - v * sum_a - average * mean_y
            slope_x = moment_yy * right_x - moment_xy * right_y
            slope_y = moment_xx * right_y - moment_xy * right_x
            s.push[f, t, pl.ds(base, 8), :] = average - slope_x * u - slope_y * v
            s.push[3 + f, t, pl.ds(base, 8), :] = slope_x
            s.push[6 + f, t, pl.ds(base, 8), :] = slope_y


def stage_push(s, tiles, west, east, base):
    lane = lane_index()
    off = [[at(s.raw, 1 + i, t, base) for t in tiles] for i in range(2)]
    west_off = [from_west(o, west, lane) for o in off]
    east_off = [from_east(o, east, lane) for o in off]
    groups = []
    for dx in (-1, 0, 1):
        seen = (west_off, off, east_off)[dx + 1]
        group = [[] for _ in range(3)]
        for k, t in enumerate(tiles):
            x = seen[0][k] + float(dx) if dx else seen[0][k]
            totals = [None] * 3
            for dy in (-1, 0, 1):
                y = seen[1][k] + float(dy) if dy else seen[1][k]
                member = at(s.mk, 3 * (dy + 1) + dx + 1, t, base, -dy)
                for f in range(3):
                    plane = at(s.push, f, t, base, -dy)
                    plane = plane + at(s.push, 3 + f, t, base, -dy) * x
                    plane = plane + at(s.push, 6 + f, t, base, -dy) * y
                    term = member * plane
                    totals[f] = term if totals[f] is None else totals[f] + term
            for f in range(3):
                group[f].append(totals[f])
        groups.append(group)
    results = []
    for f in range(3):
        low = from_east(groups[0][f], east, lane)
        high = from_west(groups[2][f], west, lane)
        results.append(
            [
                (groups[1][f][k] + low[k] + high[k]) * at(s.rc, 0, t, base)
                for k, t in enumerate(tiles)
            ]
        )
    return results


def start_all(copies):
    for copy in copies:
        copy.start()
    for copy in copies:
        copy.wait()


def pack_kernel(
    state, cut, fraction, code, flags, offset, s0, s1, p0, p1, own_rows, own_cols,
    st_r, ct_r, fr_r, cd_r, of_r, st_c, ct_c, fr_c, cd_c, of_c, mix, sem,
):
    rows = state.shape[1]
    cols = state.shape[2]
    copies = []
    for i, row in enumerate((0, rows - 8)):
        rs = pl.ds(row, 8)
        copies += [
            pltpu.make_async_copy(state.at[:, rs, :], st_r.at[i], sem.at[0, i]),
            pltpu.make_async_copy(cut.at[rs, :], ct_r.at[i], sem.at[1, i]),
            pltpu.make_async_copy(fraction.at[rs, :], fr_r.at[i], sem.at[2, i]),
            pltpu.make_async_copy(code.at[rs, :], cd_r.at[i], sem.at[3, i]),
            pltpu.make_async_copy(offset.at[:, rs, :], of_r.at[i], sem.at[4, i]),
        ]
    for i, col in enumerate((0, cols - LANES)):
        cs = pl.ds(col, LANES)
        copies += [
            pltpu.make_async_copy(state.at[:, :, cs], st_c.at[i], sem.at[5, i]),
            pltpu.make_async_copy(cut.at[:, cs], ct_c.at[i], sem.at[6, i]),
            pltpu.make_async_copy(fraction.at[:, cs], fr_c.at[i], sem.at[7, i]),
            pltpu.make_async_copy(code.at[:, cs], cd_c.at[i], sem.at[8, i]),
            pltpu.make_async_copy(offset.at[:, :, cs], of_c.at[i], sem.at[9, i]),
        ]
    start_all(copies)
    ntile = cols // LANES
    even_y = lax.rem(lax.axis_index("ty"), 2) == 0
    even_x = lax.rem(lax.axis_index("tx"), 2) == 0

    def fields(st, ct, fr, cd, of, flag):
        active = ct > (1 - flag)
        return [
            jnp.where(active, cd, 16).astype(jnp.float32),
            jnp.where(active, fr.astype(jnp.float32) * (1.0 / 1024.0), 1.0),
            jnp.where(active, of[0], 0.0),
            jnp.where(active, of[1], 0.0),
            st[0],
            st[1],
            st[2],
        ]

    mids = {}
    for t in range(ntile):
        ls = pl.ds(t * LANES, LANES)
        made = []
        for i in range(2):
            got = fields(
                st_r[i, :, :, ls], ct_r[i, :, ls], fr_r[i, :, ls], cd_r[i, :, ls], of_r[i, :, :, ls],
                flags[0, t],
            )
            for f in range(FIELDS):
                own_rows[i, f, :, ls] = got[f]
            made.append(got)
        for f in range(FIELDS):
            top = made[0][f][0:4]
            bottom = made[1][f][4:8]
            s0[pl.ds(4 * f, 4), ls] = jnp.where(even_y, bottom, top)
            s1[pl.ds(4 * f, 4), ls] = jnp.where(even_y, top, bottom)
        if t in (0, ntile - 1):
            side = 0 if t == 0 else 1
            mids[side] = made
    for side, t in enumerate((0, ntile - 1)):
        got = fields(st_c[side], ct_c[side], fr_c[side], cd_c[side], of_c[side], flags[0, t])
        first = 0 if side == 0 else LANES - 8
        for f in range(FIELDS):
            own_cols[side, f, :, :] = got[f].T[first : first + 8, :]
    for f in range(FIELDS):
        left = own_cols[0, f, 0:4, :]
        right = own_cols[1, f, 4:8, :]
        rs = pl.ds(4 * f, 4)
        p0[rs, 0:LANES] = jnp.where(even_x, right, left)
        p1[rs, 0:LANES] = jnp.where(even_x, left, right)
        for side in range(2):
            first = 0 if side == 0 else LANES - 4
            near, far = mids[side][0][f], mids[side][1][f]
            for g, piece in ((1, near[0:4]), (2, near[4:8]), (3, far[0:4]), (4, far[4:8])):
                mix[side, g, rs, :] = pltpu.roll(piece, (4 * g - first) % LANES, 1)
    lane = lax.broadcasted_iota(jnp.int32, (PACKED, LANES), 1)
    parts = []
    for side in range(2):
        total = jnp.zeros((PACKED, LANES), jnp.float32)
        for g in range(1, 5):
            here = (lane >= 4 * g) & (lane < 4 * g + 4)
            total = jnp.where(here, mix[side, g, 0:PACKED, :], total)
        parts.append(total)
    p0[:, LANES:] = jnp.where(even_x, parts[1], parts[0])
    p1[:, LANES:] = jnp.where(even_x, parts[0], parts[1])


def pack(state, cut, fraction, code, flags, offset):
    rows, cols = cut.shape
    any_spec = pl.BlockSpec(memory_space=pl.ANY)
    f32, i32 = jnp.float32, jnp.int32
    strip = lambda *s: jax.ShapeDtypeStruct(s, f32)
    return pl.pallas_call(
        pack_kernel,
        out_shape=(
            strip(PACKED, cols), strip(PACKED, cols), strip(PACKED, 2 * LANES), strip(PACKED, 2 * LANES),
            strip(2, FIELDS, 8, cols), strip(2, FIELDS, 8, rows),
        ),
        in_specs=[any_spec] * 4 + [pl.BlockSpec(memory_space=pltpu.SMEM), any_spec],
        scratch_shapes=[
            pltpu.VMEM((2, 3, 8, cols), f32),
            pltpu.VMEM((2, 8, cols), i32),
            pltpu.VMEM((2, 8, cols), i32),
            pltpu.VMEM((2, 8, cols), i32),
            pltpu.VMEM((2, 2, 8, cols), f32),
            pltpu.VMEM((2, 3, rows, LANES), f32),
            pltpu.VMEM((2, rows, LANES), i32),
            pltpu.VMEM((2, rows, LANES), i32),
            pltpu.VMEM((2, rows, LANES), i32),
            pltpu.VMEM((2, 2, rows, LANES), f32),
            pltpu.VMEM((2, 5, 32, LANES), f32),
            pltpu.SemaphoreType.DMA((10, 2)),
        ],
        compiler_params=pltpu.CompilerParams(vmem_limit_bytes=VMEM_LIMIT),
        name="pack",
    )(state, cut, fraction, code, flags, offset)


def inner_kernel(state, cut, fraction, code, flags, offset, out, ct, fr, cd, *rest):
    s = Fields(*rest[:7])
    res, sem = rest[7:]
    rows = cut.shape[0]
    ntile = cut.shape[1] // LANES
    tiles = list(range(ntile))
    west = [(t - 1) % ntile for t in tiles]
    east = [(t + 1) % ntile for t in tiles]
    own = pl.ds(8, rows)
    copies = []
    for t in tiles:
        ls = pl.ds(t * LANES, LANES)
        copies += [
            pltpu.make_async_copy(cut.at[:, ls], ct.at[t], sem.at[0, t]),
            pltpu.make_async_copy(fraction.at[:, ls], fr.at[t], sem.at[1, t]),
            pltpu.make_async_copy(code.at[:, ls], cd.at[t], sem.at[2, t]),
        ]
        for i in range(2):
            copies.append(
                pltpu.make_async_copy(offset.at[i, :, ls], s.raw.at[1 + i, t, own, :], sem.at[3 + i, t])
            )
        for f in range(3):
            copies.append(
                pltpu.make_async_copy(state.at[f, :, ls], s.raw.at[3 + f, t, own, :], sem.at[5 + f, t])
            )
    start_all(copies)
    ntr = rows // 8

    def prepare(k, carry):
        src = pl.ds(pl.multiple_of(8 * k, 8), 8)
        dst = pl.ds(pl.multiple_of(8 * k + 8, 8), 8)
        for t in tiles:
            active = ct[t, src, :] > (1 - flags[0, t])
            codes = jnp.where(active, cd[t, src, :], 16)
            kappa = jnp.where(active, fr[t, src, :].astype(jnp.float32) * (1.0 / 1024.0), 1.0)
            s.raw[0, t, dst, :] = kappa
            for i in range(2):
                s.raw[1 + i, t, dst, :] = jnp.where(active, s.raw[1 + i, t, dst, :], 0.0)
            store_members(s.mk, codes, kappa, t, dst, plain_order)
        return carry

    lax.fori_loop(0, ntr, prepare, 0)

    def share(k, carry):
        stage_share(s, tiles, west, east, 8 * k + 8)
        return carry

    def average(k, carry):
        stage_average(s, tiles, west, east, 8 * k + 8)
        return carry

    def slope(k, carry):
        stage_slope(s, tiles, 8 * k + 8)
        return carry

    def push(k, carry):
        made = stage_push(s, tiles, west, east, 8 * k + 8)
        for f in range(3):
            for t in tiles:
                res[f, pl.ds(pl.multiple_of(8 * k, 8), 8), pl.ds(t * LANES, LANES)] = made[f][t]
        return carry

    for step in (share, average, slope, push):
        lax.fori_loop(0, ntr, step, 0)
    copy = pltpu.make_async_copy(res, out, sem.at[8, 0])
    copy.start()
    copy.wait()


def inner(state, cut, fraction, code, flags, offset):
    rows, cols = cut.shape
    ntile = cols // LANES
    any_spec = pl.BlockSpec(memory_space=pl.ANY)
    ints = pltpu.VMEM((ntile, rows, LANES), jnp.int32)
    return pl.pallas_call(
        inner_kernel,
        out_shape=jax.ShapeDtypeStruct(state.shape, jnp.float32),
        in_specs=[any_spec] * 4 + [pl.BlockSpec(memory_space=pltpu.SMEM), any_spec],
        out_specs=any_spec,
        scratch_shapes=[ints, ints, ints]
        + Fields.shapes(ntile, rows + 16)
        + [pltpu.VMEM(state.shape, jnp.float32), pltpu.SemaphoreType.DMA((9, ntile))],
        compiler_params=pltpu.CompilerParams(vmem_limit_bytes=VMEM_LIMIT),
        cost_estimate=pl.CostEstimate(flops=60_000_000, transcendentals=0, bytes_accessed=3_000_000),
        name="inner",
    )(state, cut, fraction, code, flags, offset)


swap_fields = (0, 1, 3, 2, 4, 6, 5)


def rim_kernel(h0, h1, c0, c1, own_rows, own_cols, base_ref, inner_out, out, wide, *rest):
    s = Fields(*rest[:7])
    res, turn, edge_c, edge_r, sem = rest[7:]
    rows, cols = inner_out.shape[1:]
    ntile = cols // LANES
    reads = []
    for i, col in enumerate((0, cols - LANES)):
        reads.append(
            pltpu.make_async_copy(inner_out.at[:, :, pl.ds(col, LANES)], edge_c.at[i], sem.at[0, i])
        )
    for i, row in enumerate((0, rows - 8)):
        reads.append(
            pltpu.make_async_copy(
                inner_out.at[:, pl.ds(row, 8), pl.ds(LANES, cols - 2 * LANES)], edge_r.at[i], sem.at[1, i]
            )
        )
    for copy in reads:
        copy.start()
    iy, ix = lax.axis_index("ty"), lax.axis_index("tx")
    even_y, even_x = lax.rem(iy, 2) == 0, lax.rem(ix, 2) == 0
    have_top, have_bottom = iy > 0, iy < lax.axis_size("ty") - 1
    have_left, have_right = ix > 0, ix < lax.axis_size("tx") - 1
    group = ntile + 1
    top, bottom, left, right = 0, group, 2 * group, 2 * group + 1
    zero4 = jnp.zeros((4, LANES), jnp.float32)
    halo = lambda even, a, b, have: jnp.where(have, jnp.where(even, a, b), zero4)
    for f in range(FIELDS):
        rs = pl.ds(4 * f, 4)
        for t in range(ntile):
            ls = pl.ds(t * LANES, LANES)
            wide[f, top + t, 0:4, :] = halo(even_y, h1[rs, ls], h0[rs, ls], have_top)
            wide[f, top + t, 4:12, :] = own_rows[0, f, :, ls]
            wide[f, bottom + t, 0:8, :] = own_rows[1, f, :, ls]
            wide[f, bottom + t, 8:12, :] = halo(even_y, h0[rs, ls], h1[rs, ls], have_bottom)
        fe = swap_fields[f]
        wide[fe, left, 0:4, :] = halo(even_x, c1[rs, 0:LANES], c0[rs, 0:LANES], have_left)
        wide[fe, left, 4:12, :] = own_cols[0, f, :, :]
        wide[fe, right, 0:8, :] = own_cols[1, f, :, :]
        wide[fe, right, 8:12, :] = halo(even_x, c0[rs, 0:LANES], c1[rs, 0:LANES], have_right)
    lane = lax.broadcasted_iota(jnp.int32, (PACKED, LANES), 1)
    none = jnp.zeros((PACKED, LANES), jnp.float32)
    a, b = c0[:, LANES:], c1[:, LANES:]
    from_left = jnp.where(have_left, jnp.where(even_x, b, a), none)
    from_right = jnp.where(have_right, jnp.where(even_x, a, b), none)
    for g in range(6):
        l = pltpu.roll(from_left, LANES - 4 - 4 * g, 1)
        r = pltpu.roll(from_right, (LANES - 4 * g) % LANES, 1)
        both = jnp.where(lane < 4, r, jnp.where(lane >= LANES - 4, l, 0.0))
        strip, first = ((top, 4 * g) if g < 3 else (bottom, 4 * (g - 3)))
        for f in range(FIELDS):
            wide[f, strip + ntile, first : first + 4, :] = both[4 * f : 4 * f + 4, :]

    tiles = list(range(2 * group + 2))
    west, east = list(tiles), list(tiles)
    for first in (top, bottom):
        for t in range(group):
            west[first + t] = first + (t - 1) % group
            east[first + t] = first + (t + 1) % group
    base = base_ref[0]
    for t in tiles:
        order = plain_order if t < left else swapped_order
        for r in range(2):
            rs = pl.ds(8 * r, 8)
            kappa = wide[1, t, rs, :]
            store_members(s.mk, wide[0, t, rs, :].astype(jnp.int32), kappa, t, rs, order)
            s.raw[0, t, rs, :] = kappa
            for f in range(2, FIELDS):
                s.raw[f - 1, t, rs, :] = wide[f, t, rs, :]
    for first in (0, 5, 10):
        pick = tiles[first : first + 5]
        w = [west[t] - first for t in pick]
        e = [east[t] - first for t in pick]
        stage_share(s, pick, w, e, base + 1)
        stage_share(s, pick, w, e, base + 9)
        stage_average(s, pick, w, e, base + 2)
        stage_slope(s, pick, base + 3)
        made = stage_push(s, pick, w, e, base + 4)
        for f in range(3):
            for k, t in enumerate(pick):
                res[f, t, :, :] = made[f][k]
    for copy in reads:
        copy.wait()
    turn[...] = jnp.zeros_like(turn)
    for f in range(3):
        fe = (0, 2, 1)[f]
        turn[pl.ds(4 * f, 4), :] = res[fe, left, 0:4, :]
        turn[pl.ds(16 + 4 * f, 4), :] = res[fe, right, 0:4, :]
    back = turn[...].T
    lane = lax.broadcasted_iota(jnp.int32, (rows, LANES), 1)
    for f in range(3):
        edge_c[0, f] = jnp.where(lane < 4, pltpu.roll(back, (LANES - 4 * f) % LANES, 1), edge_c[0, f])
        edge_c[1, f] = jnp.where(
            lane >= LANES - 4, pltpu.roll(back, LANES - 4 - 16 - 4 * f, 1), edge_c[1, f]
        )
        for i, t in enumerate((0, ntile - 1)):
            edge_c[i, f, 0:4, :] = res[f, top + t, 0:4, :]
            edge_c[i, f, rows - 4 : rows, :] = res[f, bottom + t, 0:4, :]
        for t in range(1, ntile - 1):
            ls = pl.ds((t - 1) * LANES, LANES)
            edge_r[0, f, 0:4, ls] = res[f, top + t, 0:4, :]
            edge_r[1, f, 4:8, ls] = res[f, bottom + t, 0:4, :]
    writes = []
    for i, col in enumerate((0, cols - LANES)):
        writes.append(
            pltpu.make_async_copy(edge_c.at[i], out.at[:, :, pl.ds(col, LANES)], sem.at[0, i])
        )
    for i, row in enumerate((0, rows - 8)):
        writes.append(
            pltpu.make_async_copy(
                edge_r.at[i], out.at[:, pl.ds(row, 8), pl.ds(LANES, cols - 2 * LANES)], sem.at[1, i]
            )
        )
    start_all(writes)


def rim(h0, h1, c0, c1, own_rows, own_cols, inner_out):
    rows, cols = inner_out.shape[1:]
    ntile = cols // LANES
    tiles = 2 * (ntile + 1) + 2
    any_spec = pl.BlockSpec(memory_space=pl.ANY)
    vmem = pl.BlockSpec(memory_space=pltpu.VMEM)
    f32 = jnp.float32
    return pl.pallas_call(
        rim_kernel,
        out_shape=jax.ShapeDtypeStruct(inner_out.shape, f32),
        in_specs=[vmem] * 6 + [pl.BlockSpec(memory_space=pltpu.SMEM), any_spec],
        out_specs=any_spec,
        input_output_aliases={7: 0},
        scratch_shapes=[pltpu.VMEM((FIELDS, tiles, 16, LANES), f32)]
        + Fields.shapes(tiles, 24)
        + [
            pltpu.VMEM((3, tiles, 8, LANES), f32),
            pltpu.VMEM((LANES, LANES), f32),
            pltpu.VMEM((2, 3, rows, LANES), f32),
            pltpu.VMEM((2, 3, 8, cols - 2 * LANES), f32),
            pltpu.SemaphoreType.DMA((2, 2)),
        ],
        compiler_params=pltpu.CompilerParams(vmem_limit_bytes=VMEM_LIMIT),
        cost_estimate=pl.CostEstimate(flops=10_000_000, transcendentals=0, bytes_accessed=1_000_000),
        name="rim",
    )(h0, h1, c0, c1, own_rows, own_cols, jnp.zeros((1,), jnp.int32), inner_out)


def with_corners(payload, right_side, top, bottom):
    cols = top.shape[1]
    pick = lambda h: jnp.where(right_side, h[:, cols - 4 :], h[:, :4])
    above = jnp.pad(pick(top), ((0, 0), (LANES, LANES - 4)))
    below = jnp.pad(pick(bottom), ((0, 0), (LANES + 20, LANES - 24)))
    return payload + above + below


def body(state, cut_mask, fraction, neighbourhood, tile_flags, centroid_offset):
    args = (state, cut_mask, fraction, neighbourhood, tile_flags, centroid_offset)
    iy, ix = lax.axis_index("ty"), lax.axis_index("tx")
    even_y, even_x = iy % 2 == 0, ix % 2 == 0
    s0, s1, p0, p1, own_rows, own_cols = pack(*args)
    h0 = paired(s0, "ty", "tx", 0)
    h1 = paired(s1, "ty", "tx", 1)
    inner_out = inner(*args)
    top = jnp.where(even_y, h1, h0) * (iy > 0).astype(jnp.float32)
    bottom = jnp.where(even_y, h0, h1) * (iy < lax.axis_size("ty") - 1).astype(jnp.float32)
    c0 = paired(with_corners(p0, even_x, top, bottom), "tx", "ty", 0)
    c1 = paired(with_corners(p1, ~even_x, top, bottom), "tx", "ty", 1)
    return rim(h0, h1, c0, c1, own_rows, own_cols, inner_out)


def solution(mesh):
    placed = (
        P(None, "ty", "tx"),
        P("ty", "tx"),
        P("ty", "tx"),
        P("ty", "tx"),
        P("ty", "tx"),
        P(None, "ty", "tx"),
    )
    return jax.shard_map(
        body, mesh=mesh, in_specs=placed, out_specs=P(None, "ty", "tx"), check_vma=False
    )
```

time: 96.6 us -> 42.1 us (0.44)
  the two profiles are of different devices: /device:TPU:103 before, /device:TPU:24 now
where the time goes in v1:
time: 42.1 us; the launch traced here: 41.7 us
  Pallas kernels  23.7 us (56%)
  starting transfers between devices  9.9 us (24%)
  waiting for transfers between devices  5.33 us (13%)
  local copies, waits for them, and re-layouts  2.52 us (6%)
    pallas_call x1, Pallas kernels, inner(): pl.pallas_call(inner_kernel, out_shape=jax.ShapeDtypeStruct(state.shape,...  15.3 us
    ppermute x4, starting transfers between devices, paired(): return lax.ppermute(value, ('ty', 'tx'), sorted(pairs))  9.9 us
    ppermute x4, waiting for transfers between devices, paired(): return lax.ppermute(value, ('ty', 'tx'), sorted(pairs))  5.33 us
    pallas_call x1, Pallas kernels, rim(): pl.pallas_call(rim_kernel, out_shape=jax.ShapeDtypeStruct(inner_out.shape...  4.92 us
    pallas_call x1, Pallas kernels, pack(): pl.pallas_call(pack_kernel, out_shape=(strip(PACKED, cols), strip(PACKED,...  3.41 us
    unnamed x12, local copies, waits for them, and re-layouts  2.52 us
  transfers between devices with their start and end apart: 4, of which 2 were waited for; matrix products, arithmetic and copies ran while one was open for 0% of the time, Pallas kernels for 37%

profile of v1, /device:TPU:24, one launch (start us, length us, event | category | flops | bytes accessed | tf_op | source)
XLA Modules:
  0.0 41.7 jit_solution(4581332312825470017)
XLA Ops:
  0.0 3.4 %pack.1 = (f32[28,512]{1,0:T(8,128)}, f32[28,512]{1,0:T(8,128)}, f32[28,256]{1,0:T(8,128)}, f32[28,256]{1,0:T(8,128)}, f32[2,7,8,512]{3,2,1,0:T(8,128)}, /*index=5*/f32[2,7,8,128]{3,2,1,0:T(8,128)}) custom-call(f32[3,128,512]{2,1,0:T(8,128)} %state.3, s32[128,512]{1,0:T(8,128)} %cut.3, s32[128,512]{1,0:T(8,128)} %fraction.3, s32[128,512]{1,0:T(8,128)} %code.3, ...), custom_call_target="tpu_custom_call" | custom-call | tf_op jit(solution)/shard_map/pack/pallas_call | solution.py:341
  3.4 1.6 %collective-permute-start = (f32[28,512]{1,0:T(8,128)}, f32[28,512]{1,0:T(8,128)S(1)}, u32[]{:S(2)}, u32[]{:S(2)}) collective-permute-start(f32[28,512]{1,0:T(8,128)} %get-tuple-element.11), channel_id=1, source_target_pairs={{0,32},{1,33},{2,34},{3,35},{4,36},{5,37},{6,38},{7,39},{8,40},{9,... | collective-permute-start | bytes 172040 | tf_op jit(solution)/shard_map/ppermute | solution.py:33
  5.0 2.8 %collective-permute-start.1 = (f32[28,512]{1,0:T(8,128)}, f32[28,512]{1,0:T(8,128)S(1)}, u32[]{:S(2)}, u32[]{:S(2)}) collective-permute-start(f32[28,512]{1,0:T(8,128)} %get-tuple-element.12), channel_id=1, source_target_pairs={{0,1},{1,0},{2,3},{3,2},{4,5},{5,4},{6,7},{7,6},{8,9},{9,8},{10,11... | collective-permute-start | bytes 172040 | tf_op jit(solution)/shard_map/ppermute | solution.py:33
  7.8 0.2 collective-permute-done.h0
  8.0 0.0 copy-start
  8.0 5.1 %collective-permute-done.1.h1 = f32[28,512]{1,0:T(8,128)S(1)} collective-permute-done((f32[28,512]{1,0:T(8,128)}, f32[28,512]{1,0:T(8,128)S(1)}, u32[]{:S(2)}, u32[]{:S(2)}) %collective-permute-start.1) | collective-permute-done | bytes 57376 | tf_op jit(solution)/shard_map/ppermute | solution.py:33
  13.1 0.0 copy-start.1
  13.1 0.0 copy-done
  13.1 0.6 %copy-done.1 = f32[28,512]{1,0:T(8,128)} copy-done((f32[28,512]{1,0:T(8,128)}, f32[28,512]{1,0:T(8,128)S(1)}, u32[]{:S(2)}) %copy-start.1) | copy-done | bytes 57368
  13.7 0.0 copy-start.5
  13.7 0.1 slice_select_fusion
  13.8 0.7 %copy-done.5 = f32[28,256]{1,0:T(8,128)S(1)} copy-done((f32[28,256]{1,0:T(8,128)S(1)}, f32[28,256]{1,0:T(8,128)}, u32[]{:S(2)}) %copy-start.5) | copy-done | bytes 28696
  14.5 0.0 copy-start.4
  14.5 0.1 pad_add_fusion.1
  14.5 0.0 collective-permute-start.2
  14.6 0.6 %copy-done.4 = f32[28,256]{1,0:T(8,128)S(1)} copy-done((f32[28,256]{1,0:T(8,128)S(1)}, f32[28,256]{1,0:T(8,128)}, u32[]{:S(2)}) %copy-start.4) | copy-done | bytes 28696
  15.2 0.1 pad_add_fusion
  15.3 5.5 %collective-permute-start.3 = (f32[28,256]{1,0:T(8,128)S(1)}, f32[28,256]{1,0:T(8,128)S(1)}, u32[]{:S(2)}, u32[]{:S(2)}) collective-permute-start(f32[28,256]{1,0:T(8,128)S(1)} %pad_add_fusion), channel_id=1, source_target_pairs={{0,32},{1,2},{2,1},{3,4},{4,3},{5,6},{6,5},{7,8},{8,7},{9,10},{10,... | collective-permute-start | bytes 86024 | tf_op jit(solution)/shard_map/ppermute | solution.py:33
  20.8 15.3 %inner.1.inner_out = f32[3,128,512]{2,1,0:T(8,128)} custom-call(f32[3,128,512]{2,1,0:T(8,128)} %state.3, s32[128,512]{1,0:T(8,128)} %cut.3, s32[128,512]{1,0:T(8,128)} %fraction.3, s32[128,512]{1,0:T(8,128)} %code.3, s32[1,4]{1,0:T(1,128)} %flags.3, f32[2,128,512]{2,1,0:T(8,128)} %offset.3), custom_call_target="tpu_custom_call" | custom-call | flops 60000000 | bytes 3000000 | tf_op jit(solution)/shard_map/inner/pallas_call | solution.py:441
  36.2 0.0 collective-permute-done.2.c0
  36.2 0.0 copy-start.2
  36.2 0.0 collective-permute-done.3.c1
  36.2 0.0 copy-start.3
  36.2 0.6 %copy-done.2 = f32[28,256]{1,0:T(8,128)} copy-done((f32[28,256]{1,0:T(8,128)}, f32[28,256]{1,0:T(8,128)S(1)}, u32[]{:S(2)}) %copy-start.2) | copy-done | bytes 28696
  36.8 0.0 copy-done.3
  36.8 4.9 %rim.1 = f32[3,128,512]{2,1,0:T(8,128)} custom-call(f32[28,512]{1,0:T(8,128)} %copy-done, f32[28,512]{1,0:T(8,128)} %copy-done.1, f32[28,256]{1,0:T(8,128)} %copy-done.2, f32[28,256]{1,0:T(8,128)} %copy-done.3, f32[2,7,8,512]{3,2,1,0:T(8,128)} %get-tuple-element.15.own_rows, ...), custom_call_target="tpu_custom_call", output_to_operand_aliasing={{}: (7, {})} | custom-call | flops 10000000 | bytes 1000000 | tf_op jit(solution)/shard_map/rim/pallas_call | solution.py:580
  (1 shorter events, 0.0 us)
Async XLA Ops:
  3.4 4.6 %collective-permute-start = (f32[28,512]{1,0:T(8,128)}, f32[28,512]{1,0:T(8,128)S(1)}, u32[]{:S(2)}, u32[]{:S(2)}) collective-permute-start(f32[28,512]{1,0:T(8,128)} %get-tuple-element.11), channel_id=1, source_target_pairs={{0,32},{1,33},{2,34},{3,35},{4,36},{5,37},{6,38},{7,39},{8,40},{9,... | collective-permute-start | bytes 172040 | tf_op jit(solution)/shard_map/ppermute | solution.py:33
  5.0 8.1 %collective-permute-start.1 = (f32[28,512]{1,0:T(8,128)}, f32[28,512]{1,0:T(8,128)S(1)}, u32[]{:S(2)}, u32[]{:S(2)}) collective-permute-start(f32[28,512]{1,0:T(8,128)} %get-tuple-element.12), channel_id=1, source_target_pairs={{0,1},{1,0},{2,3},{3,2},{4,5},{5,4},{6,7},{7,6},{8,9},{9,8},{10,11... | collective-permute-start | bytes 172040 | tf_op jit(solution)/shard_map/ppermute | solution.py:33
  8.0 5.1 %copy-start = (f32[28,512]{1,0:T(8,128)}, f32[28,512]{1,0:T(8,128)S(1)}, u32[]{:S(2)}) copy-start(f32[28,512]{1,0:T(8,128)S(1)} %collective-permute-done.h0) | copy-start | bytes 172036
  13.1 0.6 %copy-start.1 = (f32[28,512]{1,0:T(8,128)}, f32[28,512]{1,0:T(8,128)S(1)}, u32[]{:S(2)}) copy-start(f32[28,512]{1,0:T(8,128)S(1)} %collective-permute-done.1.h1) | copy-start | bytes 172036
  13.7 0.8 %copy-start.5 = (f32[28,256]{1,0:T(8,128)S(1)}, f32[28,256]{1,0:T(8,128)}, u32[]{:S(2)}) copy-start(f32[28,256]{1,0:T(8,128)} %get-tuple-element.13) | copy-start | bytes 86020
  14.5 0.8 %copy-start.4 = (f32[28,256]{1,0:T(8,128)S(1)}, f32[28,256]{1,0:T(8,128)}, u32[]{:S(2)}) copy-start(f32[28,256]{1,0:T(8,128)} %get-tuple-element.14) | copy-start | bytes 86020
  14.5 21.6 %collective-permute-start.2 = (f32[28,256]{1,0:T(8,128)S(1)}, f32[28,256]{1,0:T(8,128)S(1)}, u32[]{:S(2)}, u32[]{:S(2)}) collective-permute-start(f32[28,256]{1,0:T(8,128)S(1)} %pad_add_fusion.1), channel_id=1, source_target_pairs={{0,1},{1,0},{2,3},{3,2},{4,5},{5,4},{6,7},{7,6},{8,9},{9,8},{10,11... | collective-permute-start | bytes 86024 | tf_op jit(solution)/shard_map/ppermute | solution.py:33
  15.3 20.9 %collective-permute-start.3 = (f32[28,256]{1,0:T(8,128)S(1)}, f32[28,256]{1,0:T(8,128)S(1)}, u32[]{:S(2)}, u32[]{:S(2)}) collective-permute-start(f32[28,256]{1,0:T(8,128)S(1)} %pad_add_fusion), channel_id=1, source_target_pairs={{0,32},{1,2},{2,1},{3,4},{4,3},{5,6},{6,5},{7,8},{8,7},{9,10},{10,... | collective-permute-start | bytes 86024 | tf_op jit(solution)/shard_map/ppermute | solution.py:33
  36.2 0.6 %copy-start.2 = (f32[28,256]{1,0:T(8,128)}, f32[28,256]{1,0:T(8,128)S(1)}, u32[]{:S(2)}) copy-start(f32[28,256]{1,0:T(8,128)S(1)} %collective-permute-done.2.c0) | copy-start | bytes 86020
  36.2 0.6 %copy-start.3 = (f32[28,256]{1,0:T(8,128)}, f32[28,256]{1,0:T(8,128)S(1)}, u32[]{:S(2)}) copy-start(f32[28,256]{1,0:T(8,128)S(1)} %collective-permute-done.3.c1) | copy-start | bytes 86020

commit v2 on v1

--- a/solution.py
+++ b/solution.py
@@ -11,7 +11,8 @@
 LANES = 128
 FIELDS = 7
 PACKED = 4 * FIELDS
-VMEM_LIMIT = 56 * 1024 * 1024
+MIB = 1024 * 1024
+SPLIT = 7
 
 courant = 0.1
 
@@ -67,14 +68,14 @@
 
 
 class Fields:
-    def __init__(self, mk, raw, rc, gath, cent, horiz, push):
-        self.mk, self.raw, self.rc = mk, raw, rc
+    def __init__(self, mk, raw, rc, seen, gath, cent, horiz, push):
+        self.mk, self.raw, self.rc, self.seen = mk, raw, rc, seen
         self.gath, self.cent, self.horiz, self.push = gath, cent, horiz, push
 
     @staticmethod
     def shapes(tiles, rows):
         shape = lambda n: pltpu.VMEM((n, tiles, rows, LANES), jnp.float32)
-        return [shape(9), shape(6), shape(1), shape(18), shape(5), shape(14), shape(9)]
+        return [shape(9), shape(6), shape(1), shape(4), shape(18), shape(5), shape(14), shape(9)]
 
 
 def at(ref, i, t, base, step=0):
@@ -98,6 +99,13 @@
     centre = [[at(s.raw, 3 + f, t, base) for t in tiles] for f in range(3)]
     easts = [from_east(c, east, lane) for c in centre]
     wests = [from_west(c, west, lane) for c in centre]
+    for i, move, step in ((0, from_west, -1.0), (1, from_east, 1.0)):
+        beside = west if i == 0 else east
+        x = move([at(s.raw, 1, t, base) for t in tiles], beside, lane)
+        y = move([at(s.raw, 2, t, base) for t in tiles], beside, lane)
+        for k, t in enumerate(tiles):
+            s.seen[i, t, pl.ds(base, 8), :] = x[k] + step
+            s.seen[2 + i, t, pl.ds(base, 8), :] = y[k]
     outs = [[] for _ in range(6)]
     for k, t in enumerate(tiles):
         coverage = jnp.maximum(sums[1][k] + low[k] + high[k], 0.125)
@@ -127,9 +135,7 @@
             s.gath[3 * f + 2, t, pl.ds(base, 8), :] = e[k]
 
 
-def stage_average(s, tiles, west, east, base):
-    lane = lane_index()
-    results = [[] for _ in range(5)]
+def stage_average(s, tiles, base):
     for t in tiles:
         weight = {}
         for dy in (-1, 0, 1):
@@ -148,9 +154,12 @@
                     sums[f] = term if sums[f] is None else sums[f] + term
         inv = inverse(jnp.maximum(total, 1e-3))
         for f in range(5):
-            value = sums[f] * inv
-            s.cent[f, t, pl.ds(base, 8), :] = value
-            results[f].append(value)
+            s.cent[f, t, pl.ds(base, 8), :] = sums[f] * inv
+
+
+def stage_horizontal(s, tiles, west, east, base):
+    lane = lane_index()
+    results = [[at(s.cent, f, t, base) for t in tiles] for f in range(5)]
     w = [from_west(r, west, lane) for r in results]
     e = [from_east(r, east, lane) for r in results]
     for k, t in enumerate(tiles):
@@ -201,18 +210,16 @@
 
 def stage_push(s, tiles, west, east, base):
     lane = lane_index()
-    off = [[at(s.raw, 1 + i, t, base) for t in tiles] for i in range(2)]
-    west_off = [from_west(o, west, lane) for o in off]
-    east_off = [from_east(o, east, lane) for o in off]
-    groups = []
-    for dx in (-1, 0, 1):
-        seen = (west_off, off, east_off)[dx + 1]
-        group = [[] for _ in range(3)]
-        for k, t in enumerate(tiles):
-            x = seen[0][k] + float(dx) if dx else seen[0][k]
+    groups = [[[] for _ in range(3)] for _ in range(3)]
+    for t in tiles:
+        for dx in (-1, 0, 1):
+            if dx:
+                x, middle = at(s.seen, (dx + 1) // 2, t, base), at(s.seen, 2 + (dx + 1) // 2, t, base)
+            else:
+                x, middle = at(s.raw, 1, t, base), at(s.raw, 2, t, base)
             totals = [None] * 3
             for dy in (-1, 0, 1):
-                y = seen[1][k] + float(dy) if dy else seen[1][k]
+                y = middle + float(dy) if dy else middle
                 member = at(s.mk, 3 * (dy + 1) + dx + 1, t, base, -dy)
                 for f in range(3):
                     plane = at(s.push, f, t, base, -dy)
@@ -221,8 +228,7 @@
                     term = member * plane
                     totals[f] = term if totals[f] is None else totals[f] + term
             for f in range(3):
-                group[f].append(totals[f])
-        groups.append(group)
+                groups[dx + 1][f].append(totals[f])
     results = []
     for f in range(3):
         low = from_east(groups[0][f], east, lane)
@@ -244,45 +250,40 @@
 
 
 def pack_kernel(
-    state, cut, fraction, code, flags, offset, s0, s1, p0, p1, own_rows, own_cols,
-    st_r, ct_r, fr_r, cd_r, of_r, st_c, ct_c, fr_c, cd_c, of_c, mix, sem,
+    state_in, cut_in, fraction_in, code_in, flags, offset_in,
+    s0, s1, p0, p1, own_rows, own_cols, state, cut, fraction, code, offset, mix, sem,
 ):
-    rows = state.shape[1]
-    cols = state.shape[2]
-    copies = []
-    for i, row in enumerate((0, rows - 8)):
-        rs = pl.ds(row, 8)
-        copies += [
-            pltpu.make_async_copy(state.at[:, rs, :], st_r.at[i], sem.at[0, i]),
-            pltpu.make_async_copy(cut.at[rs, :], ct_r.at[i], sem.at[1, i]),
-            pltpu.make_async_copy(fraction.at[rs, :], fr_r.at[i], sem.at[2, i]),
-            pltpu.make_async_copy(code.at[rs, :], cd_r.at[i], sem.at[3, i]),
-            pltpu.make_async_copy(offset.at[:, rs, :], of_r.at[i], sem.at[4, i]),
+    rows, cols = cut.shape
+    bands = []
+    for i, rs in enumerate((pl.ds(0, 8), pl.ds(rows - 8, 8), pl.ds(8, rows - 16))):
+        pairs = [
+            (cut_in.at[rs], cut.at[rs]),
+            (code_in.at[rs], code.at[rs]),
+            (fraction_in.at[rs], fraction.at[rs]),
+            (offset_in.at[:, rs], offset.at[:, rs]),
+            (state_in.at[:, rs], state.at[:, rs]),
         ]
-    for i, col in enumerate((0, cols - LANES)):
-        cs = pl.ds(col, LANES)
-        copies += [
-            pltpu.make_async_copy(state.at[:, :, cs], st_c.at[i], sem.at[5, i]),
-            pltpu.make_async_copy(cut.at[:, cs], ct_c.at[i], sem.at[6, i]),
-            pltpu.make_async_copy(fraction.at[:, cs], fr_c.at[i], sem.at[7, i]),
-            pltpu.make_async_copy(code.at[:, cs], cd_c.at[i], sem.at[8, i]),
-            pltpu.make_async_copy(offset.at[:, :, cs], of_c.at[i], sem.at[9, i]),
-        ]
-    start_all(copies)
+        bands.append([pltpu.make_async_copy(a, b, sem.at[i, j]) for j, (a, b) in enumerate(pairs)])
+    for band in bands:
+        for copy in band:
+            copy.start()
+    for band in bands[:2]:
+        for copy in band:
+            copy.wait()
     ntile = cols // LANES
     even_y = lax.rem(lax.axis_index("ty"), 2) == 0
     even_x = lax.rem(lax.axis_index("tx"), 2) == 0
 
-    def fields(st, ct, fr, cd, of, flag):
-        active = ct > (1 - flag)
+    def fields(rs, ls, flag):
+        active = cut[rs, ls] > (1 - flag)
         return [
-            jnp.where(active, cd, 16).astype(jnp.float32),
-            jnp.where(active, fr.astype(jnp.float32) * (1.0 / 1024.0), 1.0),
-            jnp.where(active, of[0], 0.0),
-            jnp.where(active, of[1], 0.0),
-            st[0],
-            st[1],
-            st[2],
+            jnp.where(active, code[rs, ls], 16).astype(jnp.float32),
+            jnp.where(active, fraction[rs, ls].astype(jnp.float32) * (1.0 / 1024.0), 1.0),
+            jnp.where(active, offset[0, rs, ls], 0.0),
+            jnp.where(active, offset[1, rs, ls], 0.0),
+            state[0, rs, ls],
+            state[1, rs, ls],
+            state[2, rs, ls],
         ]
 
     mids = {}
@@ -290,10 +291,7 @@
         ls = pl.ds(t * LANES, LANES)
         made = []
         for i in range(2):
-            got = fields(
-                st_r[i, :, :, ls], ct_r[i, :, ls], fr_r[i, :, ls], cd_r[i, :, ls], of_r[i, :, :, ls],
-                flags[0, t],
-            )
+            got = fields(pl.ds(i * (rows - 8), 8), ls, flags[0, t])
             for f in range(FIELDS):
                 own_rows[i, f, :, ls] = got[f]
             made.append(got)
@@ -305,8 +303,10 @@
         if t in (0, ntile - 1):
             side = 0 if t == 0 else 1
             mids[side] = made
+    for copy in bands[2]:
+        copy.wait()
     for side, t in enumerate((0, ntile - 1)):
-        got = fields(st_c[side], ct_c[side], fr_c[side], cd_c[side], of_c[side], flags[0, t])
+        got = fields(slice(None), pl.ds(t * LANES, LANES), flags[0, t])
         first = 0 if side == 0 else LANES - 8
         for f in range(FIELDS):
             own_cols[side, f, :, :] = got[f].T[first : first + 8, :]
@@ -333,86 +333,72 @@
     p1[:, LANES:] = jnp.where(even_x, parts[0], parts[1])
 
 
+def in_vmem(value):
+    return pltpu.with_memory_space_constraint(value, pltpu.VMEM)
+
+
+VMEM_SPEC = pl.BlockSpec(memory_space=pltpu.VMEM)
+SMEM_SPEC = pl.BlockSpec(memory_space=pltpu.SMEM)
+
+
 def pack(state, cut, fraction, code, flags, offset):
     rows, cols = cut.shape
-    any_spec = pl.BlockSpec(memory_space=pl.ANY)
-    f32, i32 = jnp.float32, jnp.int32
-    strip = lambda *s: jax.ShapeDtypeStruct(s, f32)
-    return pl.pallas_call(
+    strip = lambda *s: pltpu.VMEM(s, jnp.float32)
+    ints = pltpu.VMEM((rows, cols), jnp.int32)
+    hbm = pl.BlockSpec(memory_space=pltpu.HBM)
+    held = lambda a: pltpu.with_memory_space_constraint(a, pltpu.HBM)
+    made = pl.pallas_call(
         pack_kernel,
         out_shape=(
             strip(PACKED, cols), strip(PACKED, cols), strip(PACKED, 2 * LANES), strip(PACKED, 2 * LANES),
             strip(2, FIELDS, 8, cols), strip(2, FIELDS, 8, rows),
+            strip(3, rows, cols), ints, ints, ints, strip(2, rows, cols),
         ),
-        in_specs=[any_spec] * 4 + [pl.BlockSpec(memory_space=pltpu.SMEM), any_spec],
-        scratch_shapes=[
-            pltpu.VMEM((2, 3, 8, cols), f32),
-            pltpu.VMEM((2, 8, cols), i32),
-            pltpu.VMEM((2, 8, cols), i32),
-            pltpu.VMEM((2, 8, cols), i32),
-            pltpu.VMEM((2, 2, 8, cols), f32),
-            pltpu.VMEM((2, 3, rows, LANES), f32),
-            pltpu.VMEM((2, rows, LANES), i32),
-            pltpu.VMEM((2, rows, LANES), i32),
-            pltpu.VMEM((2, rows, LANES), i32),
-            pltpu.VMEM((2, 2, rows, LANES), f32),
-            pltpu.VMEM((2, 5, 32, LANES), f32),
-            pltpu.SemaphoreType.DMA((10, 2)),
-        ],
-        compiler_params=pltpu.CompilerParams(vmem_limit_bytes=VMEM_LIMIT),
+        in_specs=[hbm] * 4 + [SMEM_SPEC, hbm],
+        out_specs=[VMEM_SPEC] * 11,
+        scratch_shapes=[pltpu.VMEM((2, 5, 32, LANES), jnp.float32), pltpu.SemaphoreType.DMA((3, 5))],
+        compiler_params=pltpu.CompilerParams(vmem_limit_bytes=4 * MIB),
         name="pack",
-    )(state, cut, fraction, code, flags, offset)
-
-
-def inner_kernel(state, cut, fraction, code, flags, offset, out, ct, fr, cd, *rest):
-    s = Fields(*rest[:7])
-    res, sem = rest[7:]
-    rows = cut.shape[0]
-    ntile = cut.shape[1] // LANES
+    )(held(state), held(cut), held(fraction), held(code), flags, held(offset))
+    return [in_vmem(m) for m in made]
+
+
+def inner_kernel(first, last, state, cut, fraction, code, flags, offset, out, *rest):
+    s = Fields(*rest[:8])
+    rows, cols = cut.shape
+    ntile = cols // LANES
     tiles = list(range(ntile))
     west = [(t - 1) % ntile for t in tiles]
     east = [(t + 1) % ntile for t in tiles]
-    own = pl.ds(8, rows)
-    copies = []
-    for t in tiles:
-        ls = pl.ds(t * LANES, LANES)
-        copies += [
-            pltpu.make_async_copy(cut.at[:, ls], ct.at[t], sem.at[0, t]),
-            pltpu.make_async_copy(fraction.at[:, ls], fr.at[t], sem.at[1, t]),
-            pltpu.make_async_copy(code.at[:, ls], cd.at[t], sem.at[2, t]),
-        ]
-        for i in range(2):
-            copies.append(
-                pltpu.make_async_copy(offset.at[i, :, ls], s.raw.at[1 + i, t, own, :], sem.at[3 + i, t])
-            )
-        for f in range(3):
-            copies.append(
-                pltpu.make_async_copy(state.at[f, :, ls], s.raw.at[3 + f, t, own, :], sem.at[5 + f, t])
-            )
-    start_all(copies)
-    ntr = rows // 8
+    low, high = max(first - 1, 0), min(last + 1, rows // 8)
 
     def prepare(k, carry):
-        src = pl.ds(pl.multiple_of(8 * k, 8), 8)
+        src = pl.ds(pl.multiple_of(8 * (k + low), 8), 8)
         dst = pl.ds(pl.multiple_of(8 * k + 8, 8), 8)
         for t in tiles:
-            active = ct[t, src, :] > (1 - flags[0, t])
-            codes = jnp.where(active, cd[t, src, :], 16)
-            kappa = jnp.where(active, fr[t, src, :].astype(jnp.float32) * (1.0 / 1024.0), 1.0)
+            ls = pl.ds(t * LANES, LANES)
+            active = cut[src, ls] > (1 - flags[0, t])
+            codes = jnp.where(active, code[src, ls], 16)
+            kappa = jnp.where(active, fraction[src, ls].astype(jnp.float32) * (1.0 / 1024.0), 1.0)
             s.raw[0, t, dst, :] = kappa
             for i in range(2):
-                s.raw[1 + i, t, dst, :] = jnp.where(active, s.raw[1 + i, t, dst, :], 0.0)
+                s.raw[1 + i, t, dst, :] = jnp.where(active, offset[i, src, ls], 0.0)
+            for f in range(3):
+                s.raw[3 + f, t, dst, :] = state[f, src, ls]
             store_members(s.mk, codes, kappa, t, dst, plain_order)
         return carry
 
-    lax.fori_loop(0, ntr, prepare, 0)
-
     def share(k, carry):
-        stage_share(s, tiles, west, east, 8 * k + 8)
+        for j in range(2):
+            stage_share(s, tiles, west, east, 16 * k + 8 * j + 8)
         return carry
 
     def average(k, carry):
-        stage_average(s, tiles, west, east, 8 * k + 8)
+        stage_average(s, tiles, 8 * k + 8)
+        return carry
+
+    def horizontal(k, carry):
+        stage_horizontal(s, tiles, west, east, 8 * k + 8)
         return carry
 
     def slope(k, carry):
@@ -420,58 +406,59 @@
         return carry
 
     def push(k, carry):
-        made = stage_push(s, tiles, west, east, 8 * k + 8)
+        made = stage_push(s, tiles, west, east, 8 * (k + first - low) + 8)
         for f in range(3):
             for t in tiles:
-                res[f, pl.ds(pl.multiple_of(8 * k, 8), 8), pl.ds(t * LANES, LANES)] = made[f][t]
+                out[f, pl.ds(pl.multiple_of(8 * k, 8), 8), pl.ds(t * LANES, LANES)] = made[f][t]
         return carry
 
-    for step in (share, average, slope, push):
-        lax.fori_loop(0, ntr, step, 0)
-    copy = pltpu.make_async_copy(res, out, sem.at[8, 0])
-    copy.start()
-    copy.wait()
-
-
-def inner(state, cut, fraction, code, flags, offset):
+    count = high - low
+    lax.fori_loop(0, count, prepare, 0)
+    lax.fori_loop(0, (count + 1) // 2, share, 0)
+    for step in (average, horizontal, slope):
+        lax.fori_loop(0, count, step, 0)
+    lax.fori_loop(0, last - first, push, 0)
+
+
+def inner(first, last, state, cut, fraction, code, flags, offset):
     rows, cols = cut.shape
     ntile = cols // LANES
-    any_spec = pl.BlockSpec(memory_space=pl.ANY)
-    ints = pltpu.VMEM((ntile, rows, LANES), jnp.int32)
+    count = last - first
     return pl.pallas_call(
-        inner_kernel,
-        out_shape=jax.ShapeDtypeStruct(state.shape, jnp.float32),
-        in_specs=[any_spec] * 4 + [pl.BlockSpec(memory_space=pltpu.SMEM), any_spec],
-        out_specs=any_spec,
-        scratch_shapes=[ints, ints, ints]
-        + Fields.shapes(ntile, rows + 16)
-        + [pltpu.VMEM(state.shape, jnp.float32), pltpu.SemaphoreType.DMA((9, ntile))],
-        compiler_params=pltpu.CompilerParams(vmem_limit_bytes=VMEM_LIMIT),
-        cost_estimate=pl.CostEstimate(flops=60_000_000, transcendentals=0, bytes_accessed=3_000_000),
-        name="inner",
+        functools.partial(inner_kernel, first, last),
+        out_shape=pltpu.VMEM((3, 8 * count, cols), jnp.float32),
+        in_specs=[VMEM_SPEC] * 4 + [SMEM_SPEC, VMEM_SPEC],
+        out_specs=VMEM_SPEC,
+        scratch_shapes=Fields.shapes(ntile, 8 * count + 40),
+        cost_estimate=pl.CostEstimate(
+            flops=count * 4_000_000, transcendentals=0, bytes_accessed=count * 150_000
+        ),
+        compiler_params=pltpu.CompilerParams(vmem_limit_bytes=28 * MIB),
+        name=f"inner{first}",
     )(state, cut, fraction, code, flags, offset)
 
 
 swap_fields = (0, 1, 3, 2, 4, 6, 5)
 
 
-def rim_kernel(h0, h1, c0, c1, own_rows, own_cols, base_ref, inner_out, out, wide, *rest):
-    s = Fields(*rest[:7])
-    res, turn, edge_c, edge_r, sem = rest[7:]
-    rows, cols = inner_out.shape[1:]
+def rim_kernel(h0, h1, c0, c1, own_rows, own_cols, base_ref, low_part, high_part, out, wide, *rest):
+    s = Fields(*rest[:8])
+    res, turn, edge_c, edge_r, sem = rest[8:]
+    _, rows, cols = out.shape
     ntile = cols // LANES
-    reads = []
-    for i, col in enumerate((0, cols - LANES)):
-        reads.append(
-            pltpu.make_async_copy(inner_out.at[:, :, pl.ds(col, LANES)], edge_c.at[i], sem.at[0, i])
-        )
-    for i, row in enumerate((0, rows - 8)):
-        reads.append(
-            pltpu.make_async_copy(
-                inner_out.at[:, pl.ds(row, 8), pl.ds(LANES, cols - 2 * LANES)], edge_r.at[i], sem.at[1, i]
-            )
-        )
-    for copy in reads:
+    split = low_part.shape[1]
+    middle = pl.ds(LANES, cols - 2 * LANES)
+    early = [
+        pltpu.make_async_copy(
+            low_part.at[:, pl.ds(8, split - 8), middle], out.at[:, pl.ds(8, split - 8), middle], sem.at[2, 0]
+        ),
+        pltpu.make_async_copy(
+            high_part.at[:, pl.ds(0, rows - split - 8), middle],
+            out.at[:, pl.ds(split, rows - split - 8), middle],
+            sem.at[2, 1],
+        ),
+    ]
+    for copy in early:
         copy.start()
     iy, ix = lax.axis_index("ty"), lax.axis_index("tx")
     even_y, even_x = lax.rem(iy, 2) == 0, lax.rem(ix, 2) == 0
@@ -529,14 +516,13 @@
         e = [east[t] - first for t in pick]
         stage_share(s, pick, w, e, base + 1)
         stage_share(s, pick, w, e, base + 9)
-        stage_average(s, pick, w, e, base + 2)
+        stage_average(s, pick, base + 2)
+        stage_horizontal(s, pick, w, e, base + 2)
         stage_slope(s, pick, base + 3)
         made = stage_push(s, pick, w, e, base + 4)
         for f in range(3):
             for k, t in enumerate(pick):
                 res[f, t, :, :] = made[f][k]
-    for copy in reads:
-        copy.wait()
     turn[...] = jnp.zeros_like(turn)
     for f in range(3):
         fe = (0, 2, 1)[f]
@@ -545,10 +531,15 @@
     back = turn[...].T
     lane = lax.broadcasted_iota(jnp.int32, (rows, LANES), 1)
     for f in range(3):
-        edge_c[0, f] = jnp.where(lane < 4, pltpu.roll(back, (LANES - 4 * f) % LANES, 1), edge_c[0, f])
-        edge_c[1, f] = jnp.where(
-            lane >= LANES - 4, pltpu.roll(back, LANES - 4 - 16 - 4 * f, 1), edge_c[1, f]
-        )
+        left_cols = pltpu.roll(back, (LANES - 4 * f) % LANES, 1)
+        right_cols = pltpu.roll(back, LANES - 4 - 16 - 4 * f, 1)
+        for part, rs in ((low_part, slice(0, split)), (high_part, slice(split, rows))):
+            edge_c[0, f, rs] = jnp.where(lane[rs] < 4, left_cols[rs], part[f, :, 0:LANES])
+            edge_c[1, f, rs] = jnp.where(
+                lane[rs] >= LANES - 4, right_cols[rs], part[f, :, cols - LANES :]
+            )
+        edge_r[0, f] = low_part[f, 0:8, LANES : cols - LANES]
+        edge_r[1, f] = high_part[f, rows - split - 8 :, LANES : cols - LANES]
         for i, t in enumerate((0, ntile - 1)):
             edge_c[i, f, 0:4, :] = res[f, top + t, 0:4, :]
             edge_c[i, f, rows - 4 : rows, :] = res[f, bottom + t, 0:4, :]
@@ -568,21 +559,21 @@
             )
         )
     start_all(writes)
-
-
-def rim(h0, h1, c0, c1, own_rows, own_cols, inner_out):
-    rows, cols = inner_out.shape[1:]
+    for copy in early:
+        copy.wait()
+
+
+def rim(h0, h1, c0, c1, own_rows, own_cols, low_part, high_part):
+    cols = low_part.shape[2]
+    rows = low_part.shape[1] + high_part.shape[1]
     ntile = cols // LANES
     tiles = 2 * (ntile + 1) + 2
-    any_spec = pl.BlockSpec(memory_space=pl.ANY)
-    vmem = pl.BlockSpec(memory_space=pltpu.VMEM)
     f32 = jnp.float32
     return pl.pallas_call(
         rim_kernel,
-        out_shape=jax.ShapeDtypeStruct(inner_out.shape, f32),
-        in_specs=[vmem] * 6 + [pl.BlockSpec(memory_space=pltpu.SMEM), any_spec],
-        out_specs=any_spec,
-        input_output_aliases={7: 0},
+        out_shape=jax.ShapeDtypeStruct((3, rows, cols), f32),
+        in_specs=[VMEM_SPEC] * 6 + [SMEM_SPEC] + [VMEM_SPEC] * 2,
+        out_specs=pl.BlockSpec(memory_space=pl.ANY),
         scratch_shapes=[pltpu.VMEM((FIELDS, tiles, 16, LANES), f32)]
         + Fields.shapes(tiles, 24)
         + [
@@ -590,35 +581,60 @@
             pltpu.VMEM((LANES, LANES), f32),
             pltpu.VMEM((2, 3, rows, LANES), f32),
             pltpu.VMEM((2, 3, 8, cols - 2 * LANES), f32),
-            pltpu.SemaphoreType.DMA((2, 2)),
+            pltpu.SemaphoreType.DMA((3, 2)),
         ],
-        compiler_params=pltpu.CompilerParams(vmem_limit_bytes=VMEM_LIMIT),
         cost_estimate=pl.CostEstimate(flops=10_000_000, transcendentals=0, bytes_accessed=1_000_000),
+        compiler_params=pltpu.CompilerParams(vmem_limit_bytes=24 * MIB),
         name="rim",
-    )(h0, h1, c0, c1, own_rows, own_cols, jnp.zeros((1,), jnp.int32), inner_out)
-
-
-def with_corners(payload, right_side, top, bottom):
-    cols = top.shape[1]
-    pick = lambda h: jnp.where(right_side, h[:, cols - 4 :], h[:, :4])
-    above = jnp.pad(pick(top), ((0, 0), (LANES, LANES - 4)))
-    below = jnp.pad(pick(bottom), ((0, 0), (LANES + 20, LANES - 24)))
-    return payload + above + below
+    )(h0, h1, c0, c1, own_rows, own_cols, jnp.zeros((1,), jnp.int32), low_part, high_part)
+
+
+def corner_kernel(h0, h1, p0, p1, after, q0, q1):
+    iy, ix = lax.axis_index("ty"), lax.axis_index("tx")
+    even_y, even_x = lax.rem(iy, 2) == 0, lax.rem(ix, 2) == 0
+    have_top, have_bottom = iy > 0, iy < lax.axis_size("ty") - 1
+    cols = h0.shape[1]
+    lane = lax.broadcasted_iota(jnp.int32, (PACKED, LANES), 1)
+    corners = []
+    for first, ls in ((0, pl.ds(0, LANES)), (LANES - 4, pl.ds(cols - LANES, LANES))):
+        a, b = h0[:, ls], h1[:, ls]
+        above = jnp.where(have_top, jnp.where(even_y, b, a), 0.0)
+        below = jnp.where(have_bottom, jnp.where(even_y, a, b), 0.0)
+        above = pltpu.roll(above, (LANES - first) % LANES, 1)
+        below = pltpu.roll(below, (20 + LANES - first) % LANES, 1)
+        total = jnp.where(lane < 4, above, 0.0)
+        corners.append(jnp.where((lane >= 20) & (lane < 24), below, total))
+    left, right = corners
+    q0[:, 0:LANES] = p0[:, 0:LANES]
+    q1[:, 0:LANES] = p1[:, 0:LANES]
+    q0[:, LANES:] = p0[:, LANES:] + jnp.where(even_x, right, left)
+    q1[:, LANES:] = p1[:, LANES:] + jnp.where(even_x, left, right)
+
+
+def with_corners(h0, h1, p0, p1, after):
+    return pl.pallas_call(
+        corner_kernel,
+        out_shape=(pltpu.VMEM(p0.shape, jnp.float32), pltpu.VMEM(p1.shape, jnp.float32)),
+        in_specs=[VMEM_SPEC] * 5,
+        out_specs=[VMEM_SPEC] * 2,
+        compiler_params=pltpu.CompilerParams(vmem_limit_bytes=2 * MIB),
+        name="corner",
+    )(h0, h1, p0, p1, after)
 
 
 def body(state, cut_mask, fraction, neighbourhood, tile_flags, centroid_offset):
-    args = (state, cut_mask, fraction, neighbourhood, tile_flags, centroid_offset)
-    iy, ix = lax.axis_index("ty"), lax.axis_index("tx")
-    even_y, even_x = iy % 2 == 0, ix % 2 == 0
-    s0, s1, p0, p1, own_rows, own_cols = pack(*args)
-    h0 = paired(s0, "ty", "tx", 0)
-    h1 = paired(s1, "ty", "tx", 1)
-    inner_out = inner(*args)
-    top = jnp.where(even_y, h1, h0) * (iy > 0).astype(jnp.float32)
-    bottom = jnp.where(even_y, h0, h1) * (iy < lax.axis_size("ty") - 1).astype(jnp.float32)
-    c0 = paired(with_corners(p0, even_x, top, bottom), "tx", "ty", 0)
-    c1 = paired(with_corners(p1, ~even_x, top, bottom), "tx", "ty", 1)
-    return rim(h0, h1, c0, c1, own_rows, own_cols, inner_out)
+    s0, s1, p0, p1, own_rows, own_cols, *held = pack(
+        state, cut_mask, fraction, neighbourhood, tile_flags, centroid_offset
+    )
+    args = (*held[:4], tile_flags, held[4])
+    h0 = in_vmem(paired(s0, "ty", "tx", 0))
+    h1 = in_vmem(paired(s1, "ty", "tx", 1))
+    low_part = in_vmem(inner(0, SPLIT, *args))
+    q0, q1 = with_corners(h0, h1, p0, p1, low_part)
+    c0 = in_vmem(paired(q0, "tx", "ty", 0))
+    c1 = in_vmem(paired(q1, "tx", "ty", 1))
+    high_part = in_vmem(inner(SPLIT, state.shape[1] // 8, *args))
+    return rim(h0, h1, c0, c1, own_rows, own_cols, low_part, high_part)
 
 
 def solution(mesh):

time: 42.1 us -> 31.9 us (0.76)
  the two profiles are of different devices: /device:TPU:24 before, /device:TPU:14 now
where the time goes in v2:
time: 31.9 us; the launch traced here: 31.7 us
  Pallas kernels  19.7 us (62%)
  starting transfers between devices  10.6 us (33%)
  local copies, waits for them, and re-layouts  1.31 us (4%)
    pallas_call x2, Pallas kernels, inner(): pl.pallas_call(functools.partial(inner_kernel, first, last), out_shape=pl...  13.7 us
    ppermute x4, starting transfers between devices, paired(): return lax.ppermute(value, ('ty', 'tx'), sorted(pairs))  10.6 us
    pallas_call x1, Pallas kernels, rim(): pl.pallas_call(rim_kernel, out_shape=jax.ShapeDtypeStruct((3, rows, cols)...  3.08 us
    pallas_call x1, Pallas kernels, pack(): pl.pallas_call(pack_kernel, out_shape=(strip(PACKED, cols), strip(PACKED,...  2.8 us
    unnamed x4, local copies, waits for them, and re-layouts  1.31 us
  transfers between devices with their start and end apart: 4, of which 0 were waited for; matrix products, arithmetic and copies ran while one was open for 0% of the time, Pallas kernels for 43%

profile of v2, /device:TPU:14, one launch (start us, length us, event | category | flops | bytes accessed | tf_op | source)
XLA Modules:
  0.0 31.7 jit_solution(5568776774797714609)
XLA Ops:
  0.0 0.0 copy-start
  0.0 0.7 %copy-done = s32[1,4]{1,0:T(1,128)S(1)} copy-done((s32[1,4]{1,0:T(1,128)S(1)}, s32[1,4]{1,0:T(1,128)}, u32[]{:S(2)}) %copy-start) | copy-done | bytes 40
  0.7 2.8 %pack.1 = (f32[28,512]{1,0:T(8,128)S(1)}, f32[28,512]{1,0:T(8,128)S(1)}, f32[28,256]{1,0:T(8,128)S(1)}, f32[28,256]{1,0:T(8,128)S(1)}, f32[2,7,8,512]{3,2,1,0:T(...) custom-call(f32[3,128,512]{2,1,0:T(8,128)} %state_in.1, ...), custom_call_target="tpu_custom_call" | custom-call | tf_op jit(solution)/shard_map/pack/pallas_call | solution.py:350
  3.5 0.9 %collective-permute-start = (f32[28,512]{1,0:T(8,128)S(1)}, f32[28,512]{1,0:T(8,128)S(1)}, u32[]{:S(2)}, u32[]{:S(2)}) collective-permute-start(f32[28,512]{1,0:T(8,128)S(1)} %get-tuple-element.18), channel_id=1, source_target_pairs={{0,32},{1,33},{2,34},{3,35},{4,36},{5,37},{6,38},{7,39},{8,40},{9,... | collective-permute-start | bytes 172040 | tf_op jit(solution)/shard_map/ppermute | solution.py:34
  4.4 2.9 %collective-permute-start.1 = (f32[28,512]{1,0:T(8,128)S(1)}, f32[28,512]{1,0:T(8,128)S(1)}, u32[]{:S(2)}, u32[]{:S(2)}) collective-permute-start(f32[28,512]{1,0:T(8,128)S(1)} %get-tuple-element.19), channel_id=1, source_target_pairs={{0,1},{1,0},{2,3},{3,2},{4,5},{5,4},{6,7},{7,6},{8,9},{9,8},{10,11... | collective-permute-start | bytes 172040 | tf_op jit(solution)/shard_map/ppermute | solution.py:34
  7.3 0.0 copy-start.1
  7.3 0.7 %copy-done.1 = s32[1,4]{1,0:T(1,128)S(1)} copy-done((s32[1,4]{1,0:T(1,128)S(1)}, s32[1,4]{1,0:T(1,128)}, u32[]{:S(2)}) %copy-start.1) | copy-done | bytes 40
  7.9 6.7 %inner0.1.after.low_part = f32[3,56,512]{2,1,0:T(8,128)S(1)} custom-call(f32[3,128,512]{2,1,0:T(8,128)S(1)} %get-tuple-element.22.state, s32[128,512]{1,0:T(8,128)S(1)} %get-tuple-element.23.cut, s32[128,512]{1,0:T(8,128)S(1)} %get-tuple-element.24.fraction, s32[128,512]{1,0:T(8,128)S(1)} %get-tuple-element.25.code, s32[1,4]{1,0:T(1,128)S(1)} %copy-done.1, ...), custom_call_target="tpu_custom_call" | custom-call | flops 28000000 | bytes 1050000 | tf_op jit(solution)/shard_map/inner0/pallas_call | solution.py:427
  14.6 0.0 collective-permute-done.h0
  14.6 0.0 collective-permute-done.1.h1
  14.6 0.1 corner.1
  14.7 0.1 collective-permute-start.2
  14.8 6.7 %collective-permute-start.3 = (f32[28,256]{1,0:T(8,128)S(1)}, f32[28,256]{1,0:T(8,128)S(1)}, u32[]{:S(2)}, u32[]{:S(2)}) collective-permute-start(f32[28,256]{1,0:T(8,128)S(1)} %get-tuple-element.28), channel_id=1, source_target_pairs={{0,32},{1,2},{2,1},{3,4},{4,3},{5,6},{6,5},{7,8},{8,7},{9,10},{10,... | collective-permute-start | bytes 86024 | tf_op jit(solution)/shard_map/ppermute | solution.py:34
  21.6 7.0 %inner7.1.high_part = f32[3,72,512]{2,1,0:T(8,128)S(1)} custom-call(f32[3,128,512]{2,1,0:T(8,128)S(1)} %get-tuple-element.22.state, s32[128,512]{1,0:T(8,128)S(1)} %get-tuple-element.23.cut, s32[128,512]{1,0:T(8,128)S(1)} %get-tuple-element.24.fraction, s32[128,512]{1,0:T(8,128)S(1)} %get-tuple-element.25.code, s32[1,4]{1,0:T(1,128)S(1)} %copy-done.1, ...), custom_call_target="tpu_custom_call" | custom-call | flops 36000000 | bytes 1350000 | tf_op jit(solution)/shard_map/inner7/pallas_call | solution.py:427
  28.6 0.0 collective-permute-done.2.c0
  28.6 0.0 collective-permute-done.3.c1
  28.6 3.1 %rim.1 = f32[3,128,512]{2,1,0:T(8,128)} custom-call(f32[28,512]{1,0:T(8,128)S(1)} %collective-permute-done.h0, f32[28,512]{1,0:T(8,128)S(1)} %collective-permute-done.1.h1, f32[28,256]{1,0:T(8,128)S(1)} %collective-permute-done.2.c0, f32[28,256]{1,0:T(8,128)S(1)} %collective-permute-done.3.c1, f32[2,7,8,512]{3,2,1,0:T(8,128)S(1)} %get-tuple-element.29.own_rows, ...), custom_call_target="tpu_custom_call" | custom-call | flops 10000000 | bytes 1000000 | tf_op jit(solution)/shard_map/rim/pallas_call | solution.py:572
Async XLA Ops:
  0.0 0.7 %copy-start = (s32[1,4]{1,0:T(1,128)S(1)}, s32[1,4]{1,0:T(1,128)}, u32[]{:S(2)}) copy-start(s32[1,4]{1,0:T(1,128)} %flags.5) | copy-start | bytes 52
  3.5 11.1 %collective-permute-start = (f32[28,512]{1,0:T(8,128)S(1)}, f32[28,512]{1,0:T(8,128)S(1)}, u32[]{:S(2)}, u32[]{:S(2)}) collective-permute-start(f32[28,512]{1,0:T(8,128)S(1)} %get-tuple-element.18), channel_id=1, source_target_pairs={{0,32},{1,33},{2,34},{3,35},{4,36},{5,37},{6,38},{7,39},{8,40},{9,... | collective-permute-start | bytes 172040 | tf_op jit(solution)/shard_map/ppermute | solution.py:34
  4.4 10.2 %collective-permute-start.1 = (f32[28,512]{1,0:T(8,128)S(1)}, f32[28,512]{1,0:T(8,128)S(1)}, u32[]{:S(2)}, u32[]{:S(2)}) collective-permute-start(f32[28,512]{1,0:T(8,128)S(1)} %get-tuple-element.19), channel_id=1, source_target_pairs={{0,1},{1,0},{2,3},{3,2},{4,5},{5,4},{6,7},{7,6},{8,9},{9,8},{10,11... | collective-permute-start | bytes 172040 | tf_op jit(solution)/shard_map/ppermute | solution.py:34
  7.3 0.7 %copy-start.1 = (s32[1,4]{1,0:T(1,128)S(1)}, s32[1,4]{1,0:T(1,128)}, u32[]{:S(2)}) copy-start(s32[1,4]{1,0:T(1,128)} %flags.5) | copy-start | bytes 52
  14.7 13.9 %collective-permute-start.2 = (f32[28,256]{1,0:T(8,128)S(1)}, f32[28,256]{1,0:T(8,128)S(1)}, u32[]{:S(2)}, u32[]{:S(2)}) collective-permute-start(f32[28,256]{1,0:T(8,128)S(1)} %get-tuple-element.27), channel_id=1, source_target_pairs={{0,1},{1,0},{2,3},{3,2},{4,5},{5,4},{6,7},{7,6},{8,9},{9,8},{10,11... | collective-permute-start | bytes 86024 | tf_op jit(solution)/shard_map/ppermute | solution.py:34
  14.8 13.8 %collective-permute-start.3 = (f32[28,256]{1,0:T(8,128)S(1)}, f32[28,256]{1,0:T(8,128)S(1)}, u32[]{:S(2)}, u32[]{:S(2)}) collective-permute-start(f32[28,256]{1,0:T(8,128)S(1)} %get-tuple-element.28), channel_id=1, source_target_pairs={{0,32},{1,2},{2,1},{3,4},{4,3},{5,6},{6,5},{7,8},{8,7},{9,10},{10,... | collective-permute-start | bytes 86024 | tf_op jit(solution)/shard_map/ppermute | solution.py:34

commit v3 on v2

--- a/solution.py
+++ b/solution.py
@@ -12,7 +12,7 @@
 FIELDS = 7
 PACKED = 4 * FIELDS
 MIB = 1024 * 1024
-SPLIT = 7
+ORIGIN = 8
 
 courant = 0.1
 
@@ -249,49 +249,44 @@
         copy.wait()
 
 
+def strip_fields(state, cut, fraction, code, offset, rs, ls, limit):
+    active = cut[rs, ls] > limit
+    return [
+        jnp.where(active, code[rs, ls], 16).astype(jnp.float32),
+        jnp.where(active, fraction[rs, ls].astype(jnp.float32) * (1.0 / 1024.0), 1.0),
+        jnp.where(active, offset[0, rs, ls], 0.0),
+        jnp.where(active, offset[1, rs, ls], 0.0),
+        state[0, rs, ls],
+        state[1, rs, ls],
+        state[2, rs, ls],
+    ]
+
+
 def pack_kernel(
-    state_in, cut_in, fraction_in, code_in, flags, offset_in,
-    s0, s1, p0, p1, own_rows, own_cols, state, cut, fraction, code, offset, mix, sem,
+    state_in, cut_in, fraction_in, code_in, flags_in, offset_in,
+    s0, s1, own_rows, limit, state, cut, fraction, code, offset, flags, sem,
 ):
-    rows, cols = cut.shape
-    bands = []
-    for i, rs in enumerate((pl.ds(0, 8), pl.ds(rows - 8, 8), pl.ds(8, rows - 16))):
+    rows, cols = cut_in.shape
+    copies = [pltpu.make_async_copy(flags_in, flags, sem.at[2, 0])]
+    for i in range(2):
+        rs, to = pl.ds(i * (rows - 8), 8), pl.ds(8 * i, 8)
         pairs = [
-            (cut_in.at[rs], cut.at[rs]),
-            (code_in.at[rs], code.at[rs]),
-            (fraction_in.at[rs], fraction.at[rs]),
-            (offset_in.at[:, rs], offset.at[:, rs]),
-            (state_in.at[:, rs], state.at[:, rs]),
+            (cut_in.at[rs], cut.at[to]),
+            (code_in.at[rs], code.at[to]),
+            (fraction_in.at[rs], fraction.at[to]),
+            (offset_in.at[:, rs], offset.at[:, to]),
+            (state_in.at[:, rs], state.at[:, to]),
         ]
-        bands.append([pltpu.make_async_copy(a, b, sem.at[i, j]) for j, (a, b) in enumerate(pairs)])
-    for band in bands:
-        for copy in band:
-            copy.start()
-    for band in bands[:2]:
-        for copy in band:
-            copy.wait()
-    ntile = cols // LANES
+        copies += [pltpu.make_async_copy(a, b, sem.at[i, j]) for j, (a, b) in enumerate(pairs)]
+    start_all(copies)
     even_y = lax.rem(lax.axis_index("ty"), 2) == 0
-    even_x = lax.rem(lax.axis_index("tx"), 2) == 0
-
-    def fields(rs, ls, flag):
-        active = cut[rs, ls] > (1 - flag)
-        return [
-            jnp.where(active, code[rs, ls], 16).astype(jnp.float32),
-            jnp.where(active, fraction[rs, ls].astype(jnp.float32) * (1.0 / 1024.0), 1.0),
-            jnp.where(active, offset[0, rs, ls], 0.0),
-            jnp.where(active, offset[1, rs, ls], 0.0),
-            state[0, rs, ls],
-            state[1, rs, ls],
-            state[2, rs, ls],
-        ]
-
-    mids = {}
-    for t in range(ntile):
+    for t in range(cols // LANES):
         ls = pl.ds(t * LANES, LANES)
+        level = 1 - flags[0, t]
+        limit[:, ls] = jnp.full((8, LANES), level, jnp.int32)
         made = []
         for i in range(2):
-            got = fields(pl.ds(i * (rows - 8), 8), ls, flags[0, t])
+            got = strip_fields(state, cut, fraction, code, offset, pl.ds(8 * i, 8), ls, level)
             for f in range(FIELDS):
                 own_rows[i, f, :, ls] = got[f]
             made.append(got)
@@ -300,13 +295,61 @@
             bottom = made[1][f][4:8]
             s0[pl.ds(4 * f, 4), ls] = jnp.where(even_y, bottom, top)
             s1[pl.ds(4 * f, 4), ls] = jnp.where(even_y, top, bottom)
-        if t in (0, ntile - 1):
-            side = 0 if t == 0 else 1
-            mids[side] = made
-    for copy in bands[2]:
-        copy.wait()
+
+
+def in_vmem(value):
+    return pltpu.with_memory_space_constraint(value, pltpu.VMEM)
+
+
+def in_hbm(value):
+    return pltpu.with_memory_space_constraint(value, pltpu.HBM)
+
+
+VMEM_SPEC = pl.BlockSpec(memory_space=pltpu.VMEM)
+SMEM_SPEC = pl.BlockSpec(memory_space=pltpu.SMEM)
+HBM_SPEC = pl.BlockSpec(memory_space=pltpu.HBM)
+
+
+def pack(*args):
+    cols = args[1].shape[1]
+    f32, i32 = jnp.float32, jnp.int32
+    made = pl.pallas_call(
+        pack_kernel,
+        out_shape=(
+            pltpu.VMEM((PACKED, cols), f32), pltpu.VMEM((PACKED, cols), f32),
+            pltpu.VMEM((2, FIELDS, 8, cols), f32), pltpu.VMEM((8, cols), i32),
+        ),
+        in_specs=[HBM_SPEC] * 6,
+        out_specs=[VMEM_SPEC] * 4,
+        scratch_shapes=[
+            pltpu.VMEM((3, 16, cols), f32),
+            pltpu.VMEM((16, cols), i32),
+            pltpu.VMEM((16, cols), i32),
+            pltpu.VMEM((16, cols), i32),
+            pltpu.VMEM((2, 16, cols), f32),
+            pltpu.SMEM((1, cols // LANES), i32),
+            pltpu.SemaphoreType.DMA((3, 5)),
+        ],
+        compiler_params=pltpu.CompilerParams(vmem_limit_bytes=2 * MIB),
+        name="pack",
+    )(*[in_hbm(a) for a in args])
+    return [in_vmem(m) for m in made]
+
+
+def first_kernel(
+    state, cut, fraction, code, offset, limit, own_rows, p0, p1, own_cols, mk, raw, rc, seen, cent, gath, mix
+):
+    s = Fields(mk, raw, rc, seen, gath, cent, None, None)
+    rows, cols = cut.shape
+    ntile = cols // LANES
+    tiles = list(range(ntile))
+    west = [(t - 1) % ntile for t in tiles]
+    east = [(t + 1) % ntile for t in tiles]
+
+    even_x = lax.rem(lax.axis_index("tx"), 2) == 0
     for side, t in enumerate((0, ntile - 1)):
-        got = fields(slice(None), pl.ds(t * LANES, LANES), flags[0, t])
+        ls = pl.ds(t * LANES, LANES)
+        got = strip_fields(state, cut, fraction, code, offset, slice(None), ls, limit[0:1, ls])
         first = 0 if side == 0 else LANES - 8
         for f in range(FIELDS):
             own_cols[side, f, :, :] = got[f].T[first : first + 8, :]
@@ -317,8 +360,9 @@
         p0[rs, 0:LANES] = jnp.where(even_x, right, left)
         p1[rs, 0:LANES] = jnp.where(even_x, left, right)
         for side in range(2):
+            ls = pl.ds(side * (cols - LANES), LANES)
             first = 0 if side == 0 else LANES - 4
-            near, far = mids[side][0][f], mids[side][1][f]
+            near, far = own_rows[0, f, :, ls], own_rows[1, f, :, ls]
             for g, piece in ((1, near[0:4]), (2, near[4:8]), (3, far[0:4]), (4, far[4:8])):
                 mix[side, g, rs, :] = pltpu.roll(piece, (4 * g - first) % LANES, 1)
     lane = lax.broadcasted_iota(jnp.int32, (PACKED, LANES), 1)
@@ -332,52 +376,12 @@
     p0[:, LANES:] = jnp.where(even_x, parts[1], parts[0])
     p1[:, LANES:] = jnp.where(even_x, parts[0], parts[1])
 
-
-def in_vmem(value):
-    return pltpu.with_memory_space_constraint(value, pltpu.VMEM)
-
-
-VMEM_SPEC = pl.BlockSpec(memory_space=pltpu.VMEM)
-SMEM_SPEC = pl.BlockSpec(memory_space=pltpu.SMEM)
-
-
-def pack(state, cut, fraction, code, flags, offset):
-    rows, cols = cut.shape
-    strip = lambda *s: pltpu.VMEM(s, jnp.float32)
-    ints = pltpu.VMEM((rows, cols), jnp.int32)
-    hbm = pl.BlockSpec(memory_space=pltpu.HBM)
-    held = lambda a: pltpu.with_memory_space_constraint(a, pltpu.HBM)
-    made = pl.pallas_call(
-        pack_kernel,
-        out_shape=(
-            strip(PACKED, cols), strip(PACKED, cols), strip(PACKED, 2 * LANES), strip(PACKED, 2 * LANES),
-            strip(2, FIELDS, 8, cols), strip(2, FIELDS, 8, rows),
-            strip(3, rows, cols), ints, ints, ints, strip(2, rows, cols),
-        ),
-        in_specs=[hbm] * 4 + [SMEM_SPEC, hbm],
-        out_specs=[VMEM_SPEC] * 11,
-        scratch_shapes=[pltpu.VMEM((2, 5, 32, LANES), jnp.float32), pltpu.SemaphoreType.DMA((3, 5))],
-        compiler_params=pltpu.CompilerParams(vmem_limit_bytes=4 * MIB),
-        name="pack",
-    )(held(state), held(cut), held(fraction), held(code), flags, held(offset))
-    return [in_vmem(m) for m in made]
-
-
-def inner_kernel(first, last, state, cut, fraction, code, flags, offset, out, *rest):
-    s = Fields(*rest[:8])
-    rows, cols = cut.shape
-    ntile = cols // LANES
-    tiles = list(range(ntile))
-    west = [(t - 1) % ntile for t in tiles]
-    east = [(t + 1) % ntile for t in tiles]
-    low, high = max(first - 1, 0), min(last + 1, rows // 8)
-
     def prepare(k, carry):
-        src = pl.ds(pl.multiple_of(8 * (k + low), 8), 8)
-        dst = pl.ds(pl.multiple_of(8 * k + 8, 8), 8)
+        src = pl.ds(pl.multiple_of(8 * k, 8), 8)
+        dst = pl.ds(pl.multiple_of(8 * k + ORIGIN, 8), 8)
         for t in tiles:
             ls = pl.ds(t * LANES, LANES)
-            active = cut[src, ls] > (1 - flags[0, t])
+            active = cut[src, ls] > limit[:, ls]
             codes = jnp.where(active, code[src, ls], 16)
             kappa = jnp.where(active, fraction[src, ls].astype(jnp.float32) * (1.0 / 1024.0), 1.0)
             s.raw[0, t, dst, :] = kappa
@@ -388,78 +392,97 @@
             store_members(s.mk, codes, kappa, t, dst, plain_order)
         return carry
 
-    def share(k, carry):
-        for j in range(2):
-            stage_share(s, tiles, west, east, 16 * k + 8 * j + 8)
+    def sweep(k, carry):
+        stage_share(s, tiles, west, east, 8 * k + ORIGIN)
         return carry
 
-    def average(k, carry):
-        stage_average(s, tiles, 8 * k + 8)
+    def sweep2(k, carry):
+        stage_average(s, tiles, 8 * k + ORIGIN)
         return carry
 
-    def horizontal(k, carry):
-        stage_horizontal(s, tiles, west, east, 8 * k + 8)
+    lax.fori_loop(0, rows // 8, prepare, 0)
+    lax.fori_loop(0, rows // 8, sweep, 0)
+    lax.fori_loop(0, rows // 8, sweep2, 0)
+
+
+def second_kernel(mk, raw, rc, seen, cent, out, horiz, push):
+    s = Fields(mk, raw, rc, seen, None, cent, horiz, push)
+    ntile = mk.shape[1]
+    count = out.shape[1] // 8
+    tiles = list(range(ntile))
+    west = [(t - 1) % ntile for t in tiles]
+    east = [(t + 1) % ntile for t in tiles]
+
+    def slopes(k, carry):
+        stage_horizontal(s, tiles, west, east, 8 * k + ORIGIN)
         return carry
 
-    def slope(k, carry):
-        stage_slope(s, tiles, 8 * k + 8)
+    def slopes2(k, carry):
+        stage_slope(s, tiles, 8 * k + ORIGIN)
         return carry
 
-    def push(k, carry):
-        made = stage_push(s, tiles, west, east, 8 * (k + first - low) + 8)
+    def spread(k, carry):
+        made = stage_push(s, tiles, west, east, 8 * k + ORIGIN)
         for f in range(3):
             for t in tiles:
                 out[f, pl.ds(pl.multiple_of(8 * k, 8), 8), pl.ds(t * LANES, LANES)] = made[f][t]
         return carry
 
-    count = high - low
-    lax.fori_loop(0, count, prepare, 0)
-    lax.fori_loop(0, (count + 1) // 2, share, 0)
-    for step in (average, horizontal, slope):
-        lax.fori_loop(0, count, step, 0)
-    lax.fori_loop(0, last - first, push, 0)
-
-
-def inner(first, last, state, cut, fraction, code, flags, offset):
+    lax.fori_loop(0, count, slopes, 0)
+    lax.fori_loop(0, count, slopes2, 0)
+    lax.fori_loop(0, count, spread, 0)
+
+
+def first_part(state, cut, fraction, code, offset, limit, own_rows):
     rows, cols = cut.shape
     ntile = cols // LANES
-    count = last - first
-    return pl.pallas_call(
-        functools.partial(inner_kernel, first, last),
-        out_shape=pltpu.VMEM((3, 8 * count, cols), jnp.float32),
-        in_specs=[VMEM_SPEC] * 4 + [SMEM_SPEC, VMEM_SPEC],
-        out_specs=VMEM_SPEC,
-        scratch_shapes=Fields.shapes(ntile, 8 * count + 40),
-        cost_estimate=pl.CostEstimate(
-            flops=count * 4_000_000, transcendentals=0, bytes_accessed=count * 150_000
+    f32 = jnp.float32
+    mk, raw, rc, seen, gath, cent, _, _ = Fields.shapes(ntile, rows + 16)
+    made = pl.pallas_call(
+        first_kernel,
+        out_shape=(
+            pltpu.VMEM((PACKED, 2 * LANES), f32), pltpu.VMEM((PACKED, 2 * LANES), f32),
+            pltpu.VMEM((2, FIELDS, 8, rows), f32), mk, raw, rc, seen, cent,
         ),
-        compiler_params=pltpu.CompilerParams(vmem_limit_bytes=28 * MIB),
-        name=f"inner{first}",
-    )(state, cut, fraction, code, flags, offset)
+        in_specs=[VMEM_SPEC] * 7,
+        out_specs=[VMEM_SPEC] * 8,
+        scratch_shapes=[gath, pltpu.VMEM((2, 5, 32, LANES), f32)],
+        compiler_params=pltpu.CompilerParams(vmem_limit_bytes=10 * MIB),
+        cost_estimate=pl.CostEstimate(flops=30_000_000, transcendentals=0, bytes_accessed=1_000_000),
+        name="first",
+    )(state, cut, fraction, code, offset, limit, own_rows)
+    return [in_vmem(m) for m in made]
+
+
+def second_part(rows, *held):
+    ntile = held[0].shape[1]
+    *_, horiz, push = Fields.shapes(ntile, rows + 16)
+    return in_vmem(
+        pl.pallas_call(
+            second_kernel,
+            out_shape=pltpu.VMEM((3, rows, ntile * LANES), jnp.float32),
+            in_specs=[VMEM_SPEC] * 5,
+            out_specs=VMEM_SPEC,
+            scratch_shapes=[horiz, push],
+            compiler_params=pltpu.CompilerParams(vmem_limit_bytes=12 * MIB),
+            cost_estimate=pl.CostEstimate(flops=30_000_000, transcendentals=0, bytes_accessed=1_000_000),
+            name="second",
+        )(*held)
+    )
 
 
 swap_fields = (0, 1, 3, 2, 4, 6, 5)
 
 
-def rim_kernel(h0, h1, c0, c1, own_rows, own_cols, base_ref, low_part, high_part, out, wide, *rest):
+def rim_kernel(h0, h1, c0, c1, own_rows, own_cols, base_ref, inner_out, out, wide, *rest):
     s = Fields(*rest[:8])
-    res, turn, edge_c, edge_r, sem = rest[8:]
+    turn, edge_c, edge_r, sem = rest[8:]
     _, rows, cols = out.shape
     ntile = cols // LANES
-    split = low_part.shape[1]
+    inside = pl.ds(8, rows - 16)
     middle = pl.ds(LANES, cols - 2 * LANES)
-    early = [
-        pltpu.make_async_copy(
-            low_part.at[:, pl.ds(8, split - 8), middle], out.at[:, pl.ds(8, split - 8), middle], sem.at[2, 0]
-        ),
-        pltpu.make_async_copy(
-            high_part.at[:, pl.ds(0, rows - split - 8), middle],
-            out.at[:, pl.ds(split, rows - split - 8), middle],
-            sem.at[2, 1],
-        ),
-    ]
-    for copy in early:
-        copy.start()
+    writes = [pltpu.make_async_copy(inner_out.at[:, inside, middle], out.at[:, inside, middle], sem.at[0])]
+    writes[0].start()
     iy, ix = lax.axis_index("ty"), lax.axis_index("tx")
     even_y, even_x = lax.rem(iy, 2) == 0, lax.rem(ix, 2) == 0
     have_top, have_bottom = iy > 0, iy < lax.axis_size("ty") - 1
@@ -510,86 +533,80 @@
             s.raw[0, t, rs, :] = kappa
             for f in range(2, FIELDS):
                 s.raw[f - 1, t, rs, :] = wide[f, t, rs, :]
-    for first in (0, 5, 10):
-        pick = tiles[first : first + 5]
-        w = [west[t] - first for t in pick]
-        e = [east[t] - first for t in pick]
+    def run(pick):
+        w = [pick.index(west[t]) for t in pick]
+        e = [pick.index(east[t]) for t in pick]
         stage_share(s, pick, w, e, base + 1)
         stage_share(s, pick, w, e, base + 9)
         stage_average(s, pick, base + 2)
         stage_horizontal(s, pick, w, e, base + 2)
         stage_slope(s, pick, base + 3)
-        made = stage_push(s, pick, w, e, base + 4)
-        for f in range(3):
-            for k, t in enumerate(pick):
-                res[f, t, :, :] = made[f][k]
+        return stage_push(s, pick, w, e, base + 4)
+
+    made = run([left, right])
     turn[...] = jnp.zeros_like(turn)
     for f in range(3):
         fe = (0, 2, 1)[f]
-        turn[pl.ds(4 * f, 4), :] = res[fe, left, 0:4, :]
-        turn[pl.ds(16 + 4 * f, 4), :] = res[fe, right, 0:4, :]
+        turn[pl.ds(4 * f, 4), :] = made[fe][0][0:4]
+        turn[pl.ds(16 + 4 * f, 4), :] = made[fe][1][0:4]
     back = turn[...].T
     lane = lax.broadcasted_iota(jnp.int32, (rows, LANES), 1)
     for f in range(3):
         left_cols = pltpu.roll(back, (LANES - 4 * f) % LANES, 1)
         right_cols = pltpu.roll(back, LANES - 4 - 16 - 4 * f, 1)
-        for part, rs in ((low_part, slice(0, split)), (high_part, slice(split, rows))):
-            edge_c[0, f, rs] = jnp.where(lane[rs] < 4, left_cols[rs], part[f, :, 0:LANES])
-            edge_c[1, f, rs] = jnp.where(
-                lane[rs] >= LANES - 4, right_cols[rs], part[f, :, cols - LANES :]
-            )
-        edge_r[0, f] = low_part[f, 0:8, LANES : cols - LANES]
-        edge_r[1, f] = high_part[f, rows - split - 8 :, LANES : cols - LANES]
-        for i, t in enumerate((0, ntile - 1)):
-            edge_c[i, f, 0:4, :] = res[f, top + t, 0:4, :]
-            edge_c[i, f, rows - 4 : rows, :] = res[f, bottom + t, 0:4, :]
-        for t in range(1, ntile - 1):
-            ls = pl.ds((t - 1) * LANES, LANES)
-            edge_r[0, f, 0:4, ls] = res[f, top + t, 0:4, :]
-            edge_r[1, f, 4:8, ls] = res[f, bottom + t, 0:4, :]
-    writes = []
+        edge_c[0, f] = jnp.where(lane < 4, left_cols, inner_out[f, :, 0:LANES])
+        edge_c[1, f] = jnp.where(lane >= LANES - 4, right_cols, inner_out[f, :, cols - LANES :])
     for i, col in enumerate((0, cols - LANES)):
         writes.append(
-            pltpu.make_async_copy(edge_c.at[i], out.at[:, :, pl.ds(col, LANES)], sem.at[0, i])
-        )
-    for i, row in enumerate((0, rows - 8)):
-        writes.append(
             pltpu.make_async_copy(
-                edge_r.at[i], out.at[:, pl.ds(row, 8), pl.ds(LANES, cols - 2 * LANES)], sem.at[1, i]
+                edge_c.at[i, :, inside], out.at[:, inside, pl.ds(col, LANES)], sem.at[1 + i]
             )
         )
-    start_all(writes)
-    for copy in early:
+        writes[-1].start()
+    for i, (strip, row) in enumerate(((top, 0), (bottom, rows - 8))):
+        made = run(list(range(strip, strip + group)))
+        fresh = slice(0, 4) if i == 0 else slice(4, 8)
+        kept = slice(4, 8) if i == 0 else slice(0, 4)
+        rs = slice(row + kept.start, row + kept.stop)
+        for f in range(3):
+            for t in range(ntile):
+                ls = pl.ds(t * LANES, LANES)
+                edge_r[i, f, fresh, ls] = made[f][t][0:4]
+                if t in (0, ntile - 1):
+                    edge_r[i, f, kept, ls] = edge_c[min(t, 1), f, rs]
+                else:
+                    edge_r[i, f, kept, ls] = inner_out[f, rs, ls]
+        writes.append(pltpu.make_async_copy(edge_r.at[i], out.at[:, pl.ds(row, 8)], sem.at[3 + i]))
+        writes[-1].start()
+    for copy in writes:
         copy.wait()
 
 
-def rim(h0, h1, c0, c1, own_rows, own_cols, low_part, high_part):
-    cols = low_part.shape[2]
-    rows = low_part.shape[1] + high_part.shape[1]
+def rim(h0, h1, c0, c1, own_rows, own_cols, inner_out):
+    _, rows, cols = inner_out.shape
     ntile = cols // LANES
     tiles = 2 * (ntile + 1) + 2
     f32 = jnp.float32
     return pl.pallas_call(
         rim_kernel,
-        out_shape=jax.ShapeDtypeStruct((3, rows, cols), f32),
-        in_specs=[VMEM_SPEC] * 6 + [SMEM_SPEC] + [VMEM_SPEC] * 2,
-        out_specs=pl.BlockSpec(memory_space=pl.ANY),
+        out_shape=pltpu.HBM((3, rows, cols), f32),
+        in_specs=[VMEM_SPEC] * 6 + [SMEM_SPEC, VMEM_SPEC],
+        out_specs=HBM_SPEC,
         scratch_shapes=[pltpu.VMEM((FIELDS, tiles, 16, LANES), f32)]
         + Fields.shapes(tiles, 24)
         + [
-            pltpu.VMEM((3, tiles, 8, LANES), f32),
             pltpu.VMEM((LANES, LANES), f32),
             pltpu.VMEM((2, 3, rows, LANES), f32),
-            pltpu.VMEM((2, 3, 8, cols - 2 * LANES), f32),
-            pltpu.SemaphoreType.DMA((3, 2)),
+            pltpu.VMEM((2, 3, 8, cols), f32),
+            pltpu.SemaphoreType.DMA((5,)),
         ],
+        compiler_params=pltpu.CompilerParams(vmem_limit_bytes=16 * MIB),
         cost_estimate=pl.CostEstimate(flops=10_000_000, transcendentals=0, bytes_accessed=1_000_000),
-        compiler_params=pltpu.CompilerParams(vmem_limit_bytes=24 * MIB),
         name="rim",
-    )(h0, h1, c0, c1, own_rows, own_cols, jnp.zeros((1,), jnp.int32), low_part, high_part)
-
-
-def corner_kernel(h0, h1, p0, p1, after, q0, q1):
+    )(h0, h1, c0, c1, own_rows, own_cols, jnp.zeros((1,), jnp.int32), inner_out)
+
+
+def corner_kernel(h0, h1, p0, p1, q0, q1):
     iy, ix = lax.axis_index("ty"), lax.axis_index("tx")
     even_y, even_x = lax.rem(iy, 2) == 0, lax.rem(ix, 2) == 0
     have_top, have_bottom = iy > 0, iy < lax.axis_size("ty") - 1
@@ -611,30 +628,29 @@
     q1[:, LANES:] = p1[:, LANES:] + jnp.where(even_x, left, right)
 
 
-def with_corners(h0, h1, p0, p1, after):
+def with_corners(h0, h1, p0, p1):
     return pl.pallas_call(
         corner_kernel,
         out_shape=(pltpu.VMEM(p0.shape, jnp.float32), pltpu.VMEM(p1.shape, jnp.float32)),
-        in_specs=[VMEM_SPEC] * 5,
+        in_specs=[VMEM_SPEC] * 4,
         out_specs=[VMEM_SPEC] * 2,
         compiler_params=pltpu.CompilerParams(vmem_limit_bytes=2 * MIB),
         name="corner",
-    )(h0, h1, p0, p1, after)
+    )(h0, h1, p0, p1)
 
 
 def body(state, cut_mask, fraction, neighbourhood, tile_flags, centroid_offset):
-    s0, s1, p0, p1, own_rows, own_cols, *held = pack(
-        state, cut_mask, fraction, neighbourhood, tile_flags, centroid_offset
-    )
-    args = (*held[:4], tile_flags, held[4])
+    args = (state, cut_mask, fraction, neighbourhood, tile_flags, centroid_offset)
+    s0, s1, own_rows, limit = pack(*args)
     h0 = in_vmem(paired(s0, "ty", "tx", 0))
     h1 = in_vmem(paired(s1, "ty", "tx", 1))
-    low_part = in_vmem(inner(0, SPLIT, *args))
-    q0, q1 = with_corners(h0, h1, p0, p1, low_part)
+    held = [in_vmem(a) for a in (state, cut_mask, fraction, neighbourhood, centroid_offset)]
+    p0, p1, own_cols, *fields = first_part(*held, limit, own_rows)
+    q0, q1 = with_corners(h0, h1, p0, p1)
     c0 = in_vmem(paired(q0, "tx", "ty", 0))
     c1 = in_vmem(paired(q1, "tx", "ty", 1))
-    high_part = in_vmem(inner(SPLIT, state.shape[1] // 8, *args))
-    return rim(h0, h1, c0, c1, own_rows, own_cols, low_part, high_part)
+    inner_out = second_part(state.shape[1], *fields)
+    return rim(h0, h1, c0, c1, own_rows, own_cols, inner_out)
 
 
 def solution(mesh):

time: 31.9 us -> 27 us (0.85)
  Pallas kernels: 19.7 us -> 16.2 us
  local copies, waits for them, and re-layouts: 1.31 us -> 0.02 us
    pallas_call x4, Pallas kernels: 19.6 us -> 16.1 us  [the longest x1 5.98 us: first_part(): pl.pallas_call(first_kernel, out_shape=(pltpu.VMEM((PACKED, 2 * LANES), f...]
    unnamed x4 -> x10, local copies, waits for them, and re-layouts: 1.31 us -> 0.02 us
  transfers between devices with their start and end apart: 4 -> 4, of which waited for: 0 -> 0; matrix products, arithmetic and copies ran while one was open for 0% -> 0% of each run, Pallas kernels for 43% -> 44%
where the time goes in v3:
time: 27 us; the launch traced here: 26.9 us
  Pallas kernels  16.2 us (60%)
  starting transfers between devices  10.6 us (39%)
    ppermute x4, starting transfers between devices, paired(): return lax.ppermute(value, ('ty', 'tx'), sorted(pairs))  10.6 us
    pallas_call x1, Pallas kernels, first_part(): pl.pallas_call(first_kernel, out_shape=(pltpu.VMEM((PACKED, 2 * LANES), f...  5.98 us
    pallas_call x1, Pallas kernels, second_part(): pl.pallas_call(second_kernel, out_shape=pltpu.VMEM((3, rows, ntile * LANE...  5.77 us
    pallas_call x1, Pallas kernels, rim(): pl.pallas_call(rim_kernel, out_shape=pltpu.HBM((3, rows, cols), f32), in_...  3.07 us
    pallas_call x1, Pallas kernels, pack(): pl.pallas_call(pack_kernel, out_shape=(pltpu.VMEM((PACKED, cols), f32), p...  1.24 us
  transfers between devices with their start and end apart: 4, of which 0 were waited for; matrix products, arithmetic and copies ran while one was open for 0% of the time, Pallas kernels for 44%

profile of v3, /device:TPU:14, one launch (start us, length us, event | category | flops | bytes accessed | tf_op | source)
XLA Modules:
  0.0 26.9 jit_solution(16332429881292509064)
XLA Ops:
  0.0 0.0 copy-start.1
  0.0 0.0 copy-start.4
  0.0 0.0 copy-start.3
  0.0 0.0 copy-start.2
  0.0 0.0 copy-start
  0.0 1.2 %pack.1 = (f32[28,512]{1,0:T(8,128)S(1)}, f32[28,512]{1,0:T(8,128)S(1)}, f32[2,7,8,512]{3,2,1,0:T(8,128)S(1)}, s32[8,512]{1,0:T(8,128)S(1)}) custom-call(f32[3,128,512]{2,1,0:T(8,128)} %state.1, s32[128,512]{1,0:T(8,128)} %cut.1, s32[128,512]{1,0:T(8,128)} %fraction.1, s32[128,512]{1,0:T(8,128)} %code.1, s32[1,4]{1,0:T(1,128)} %flags_in.1, f32[2,128,512]{2,1,0:T(8,128)} %offset.1), custom_call_target="tpu_custom_call" | custom-call | tf_op jit(solution)/shard_map/pack/pallas_call | solution.py:316
  1.3 0.9 %collective-permute-start = (f32[28,512]{1,0:T(8,128)S(1)}, f32[28,512]{1,0:T(8,128)S(1)}, u32[]{:S(2)}, u32[]{:S(2)}) collective-permute-start(f32[28,512]{1,0:T(8,128)S(1)} %get-tuple-element.19), channel_id=1, source_target_pairs={{0,32},{1,33},{2,34},{3,35},{4,36},{5,37},{6,38},{7,39},{8,40},{9,... | collective-permute-start | bytes 172040 | tf_op jit(solution)/shard_map/ppermute | solution.py:34
  2.2 2.9 %collective-permute-start.1 = (f32[28,512]{1,0:T(8,128)S(1)}, f32[28,512]{1,0:T(8,128)S(1)}, u32[]{:S(2)}, u32[]{:S(2)}) collective-permute-start(f32[28,512]{1,0:T(8,128)S(1)} %get-tuple-element.20), channel_id=1, source_target_pairs={{0,1},{1,0},{2,3},{3,2},{4,5},{5,4},{6,7},{7,6},{8,9},{9,8},{10,11... | collective-permute-start | bytes 172040 | tf_op jit(solution)/shard_map/ppermute | solution.py:34
  5.1 0.0 copy-done.1
  5.1 0.0 copy-done.4
  5.1 0.0 copy-done.3
  5.1 0.0 copy-done.2
  5.1 0.0 copy-done
  5.1 6.0 %first.1 = (f32[28,256]{1,0:T(8,128)S(1)}, f32[28,256]{1,0:T(8,128)S(1)}, f32[2,7,8,128]{3,2,1,0:T(8,128)S(1)}, f32[9,4,144,128]{3,2,1,0:T(8,128)S(1)}, f32[6,4,...) custom-call(f32[3,128,512]{2,1,0:T(8,128)S(1)} %copy-done, ...), custom_call_target="tpu_custom_call" | custom-call | flops 30000000 | bytes 1000000 | tf_op jit(solution)/shard_map/first/pallas_call | solution.py:441
  11.1 0.0 collective-permute-done.h0
  11.1 0.0 collective-permute-done.1.h1
  11.1 0.1 corner.1
  11.2 0.1 collective-permute-start.2
  11.3 6.7 %collective-permute-start.3 = (f32[28,256]{1,0:T(8,128)S(1)}, f32[28,256]{1,0:T(8,128)S(1)}, u32[]{:S(2)}, u32[]{:S(2)}) collective-permute-start(f32[28,256]{1,0:T(8,128)S(1)} %get-tuple-element.26), channel_id=1, source_target_pairs={{0,32},{1,2},{2,1},{3,4},{4,3},{5,6},{6,5},{7,8},{8,7},{9,10},{10,... | collective-permute-start | bytes 86024 | tf_op jit(solution)/shard_map/ppermute | solution.py:34
  18.0 5.8 %second.1.inner_out = f32[3,128,512]{2,1,0:T(8,128)S(1)} custom-call(f32[9,4,144,128]{3,2,1,0:T(8,128)S(1)} %get-tuple-element.28.mk, f32[6,4,144,128]{3,2,1,0:T(8,128)S(1)} %get-tuple-element.29.raw, f32[1,4,144,128]{3,2,1,0:T(8,128)S(1)} %get-tuple-element.30.rc, f32[4,4,144,128]{3,2,1,0:T(8,128)S(1)} %get-tuple-element.31.seen, ...), custom_call_target="tpu_custom_call" | custom-call | flops 30000000 | bytes 1000000 | tf_op jit(solution)/shard_map/second/pallas_call | solution.py:461
  23.8 0.0 collective-permute-done.2.c0
  23.8 0.0 collective-permute-done.3.c1
  23.8 3.1 %rim.1 = f32[3,128,512]{2,1,0:T(8,128)} custom-call(f32[28,512]{1,0:T(8,128)S(1)} %collective-permute-done.h0, f32[28,512]{1,0:T(8,128)S(1)} %collective-permute-done.1.h1, f32[28,256]{1,0:T(8,128)S(1)} %collective-permute-done.2.c0, f32[28,256]{1,0:T(8,128)S(1)} %collective-permute-done.3.c1, f32[2,7,8,512]{3,2,1,0:T(8,128)S(1)} %get-tuple-element.22.own_rows, ...), custom_call_target="tpu_custom_call" | custom-call | flops 10000000 | bytes 1000000 | tf_op jit(solution)/shard_map/rim/pallas_call | solution.py:590
Async XLA Ops:
  0.0 5.1 %copy-start.1 = (f32[2,128,512]{2,1,0:T(8,128)S(1)}, f32[2,128,512]{2,1,0:T(8,128)}, u32[]{:S(2)}) copy-start(f32[2,128,512]{2,1,0:T(8,128)} %offset.1) | copy-start | bytes 1572868
  0.0 5.1 %copy-start.4 = (s32[128,512]{1,0:T(8,128)S(1)}, s32[128,512]{1,0:T(8,128)}, u32[]{:S(2)}) copy-start(s32[128,512]{1,0:T(8,128)} %code.1) | copy-start | bytes 786436
  0.0 5.1 %copy-start.3 = (s32[128,512]{1,0:T(8,128)S(1)}, s32[128,512]{1,0:T(8,128)}, u32[]{:S(2)}) copy-start(s32[128,512]{1,0:T(8,128)} %fraction.1) | copy-start | bytes 786436
  0.0 5.1 %copy-start.2 = (s32[128,512]{1,0:T(8,128)S(1)}, s32[128,512]{1,0:T(8,128)}, u32[]{:S(2)}) copy-start(s32[128,512]{1,0:T(8,128)} %cut.1) | copy-start | bytes 786436
  0.0 5.1 %copy-start = (f32[3,128,512]{2,1,0:T(8,128)S(1)}, f32[3,128,512]{2,1,0:T(8,128)}, u32[]{:S(2)}) copy-start(f32[3,128,512]{2,1,0:T(8,128)} %state.1) | copy-start | bytes 2359300
  1.3 9.8 %collective-permute-start = (f32[28,512]{1,0:T(8,128)S(1)}, f32[28,512]{1,0:T(8,128)S(1)}, u32[]{:S(2)}, u32[]{:S(2)}) collective-permute-start(f32[28,512]{1,0:T(8,128)S(1)} %get-tuple-element.19), channel_id=1, source_target_pairs={{0,32},{1,33},{2,34},{3,35},{4,36},{5,37},{6,38},{7,39},{8,40},{9,... | collective-permute-start | bytes 172040 | tf_op jit(solution)/shard_map/ppermute | solution.py:34
  2.2 8.9 %collective-permute-start.1 = (f32[28,512]{1,0:T(8,128)S(1)}, f32[28,512]{1,0:T(8,128)S(1)}, u32[]{:S(2)}, u32[]{:S(2)}) collective-permute-start(f32[28,512]{1,0:T(8,128)S(1)} %get-tuple-element.20), channel_id=1, source_target_pairs={{0,1},{1,0},{2,3},{3,2},{4,5},{5,4},{6,7},{7,6},{8,9},{9,8},{10,11... | collective-permute-start | bytes 172040 | tf_op jit(solution)/shard_map/ppermute | solution.py:34
  11.2 12.6 %collective-permute-start.2 = (f32[28,256]{1,0:T(8,128)S(1)}, f32[28,256]{1,0:T(8,128)S(1)}, u32[]{:S(2)}, u32[]{:S(2)}) collective-permute-start(f32[28,256]{1,0:T(8,128)S(1)} %get-tuple-element.25), channel_id=1, source_target_pairs={{0,1},{1,0},{2,3},{3,2},{4,5},{5,4},{6,7},{7,6},{8,9},{9,8},{10,11... | collective-permute-start | bytes 86024 | tf_op jit(solution)/shard_map/ppermute | solution.py:34
  11.3 12.5 %collective-permute-start.3 = (f32[28,256]{1,0:T(8,128)S(1)}, f32[28,256]{1,0:T(8,128)S(1)}, u32[]{:S(2)}, u32[]{:S(2)}) collective-permute-start(f32[28,256]{1,0:T(8,128)S(1)} %get-tuple-element.26), channel_id=1, source_target_pairs={{0,32},{1,2},{2,1},{3,4},{4,3},{5,6},{6,5},{7,8},{8,7},{9,10},{10,... | collective-permute-start | bytes 86024 | tf_op jit(solution)/shard_map/ppermute | solution.py:34

commit v4 on v3

--- a/solution.py
+++ b/solution.py
@@ -437,7 +437,8 @@
     rows, cols = cut.shape
     ntile = cols // LANES
     f32 = jnp.float32
-    mk, raw, rc, seen, gath, cent, _, _ = Fields.shapes(ntile, rows + 16)
+    mk, raw, rc, seen, _, cent, _, _ = Fields.shapes(ntile, rows + 16)
+    gath = Fields.shapes(ntile + 1, rows + 24)[4]
     made = pl.pallas_call(
         first_kernel,
         out_shape=(
@@ -456,7 +457,7 @@
 
 def second_part(rows, *held):
     ntile = held[0].shape[1]
-    *_, horiz, push = Fields.shapes(ntile, rows + 16)
+    *_, horiz, push = Fields.shapes(ntile + 1, rows + 24)
     return in_vmem(
         pl.pallas_call(
             second_kernel,
@@ -592,8 +593,8 @@
         out_shape=pltpu.HBM((3, rows, cols), f32),
         in_specs=[VMEM_SPEC] * 6 + [SMEM_SPEC, VMEM_SPEC],
         out_specs=HBM_SPEC,
-        scratch_shapes=[pltpu.VMEM((FIELDS, tiles, 16, LANES), f32)]
-        + Fields.shapes(tiles, 24)
+        scratch_shapes=[pltpu.VMEM((FIELDS, tiles + 1, 24, LANES), f32)]
+        + Fields.shapes(tiles + 1, 24)
         + [
             pltpu.VMEM((LANES, LANES), f32),
             pltpu.VMEM((2, 3, rows, LANES), f32),

time: 27 us -> 26.2 us (0.970)
  Pallas kernels: 16.2 us -> 15.4 us
    pallas_call x1, Pallas kernels: 5.98 us -> 5.41 us  [first_part(): pl.pallas_call(first_kernel, out_shape=(pltpu.VMEM((PACKED, 2 * LANES), f...]
    pallas_call x1, Pallas kernels: 5.77 us -> 5.45 us  [second_part(): pl.pallas_call(second_kernel, out_shape=pltpu.VMEM((3, rows, ntile * LANE...]
  transfers between devices with their start and end apart: 4 -> 4, of which waited for: 0 -> 0; matrix products, arithmetic and copies ran while one was open for 0% -> 0% of each run, Pallas kernels for 44% -> 42%
where the time goes in v4:
time: 26.2 us; the launch traced here: 26.1 us
  Pallas kernels  15.4 us (59%)
  starting transfers between devices  10.6 us (40%)
    ppermute x4, starting transfers between devices, paired(): return lax.ppermute(value, ('ty', 'tx'), sorted(pairs))  10.6 us
    pallas_call x1, Pallas kernels, second_part(): pl.pallas_call(second_kernel, out_shape=pltpu.VMEM((3, rows, ntile * LANE...  5.45 us
    pallas_call x1, Pallas kernels, first_part(): pl.pallas_call(first_kernel, out_shape=(pltpu.VMEM((PACKED, 2 * LANES), f...  5.41 us
    pallas_call x1, Pallas kernels, rim(): pl.pallas_call(rim_kernel, out_shape=pltpu.HBM((3, rows, cols), f32), in_...  3.15 us
    pallas_call x1, Pallas kernels, pack(): pl.pallas_call(pack_kernel, out_shape=(pltpu.VMEM((PACKED, cols), f32), p...  1.24 us
  transfers between devices with their start and end apart: 4, of which 0 were waited for; matrix products, arithmetic and copies ran while one was open for 0% of the time, Pallas kernels for 42%

profile of v4, /device:TPU:14, one launch (start us, length us, event | category | flops | bytes accessed | tf_op | source)
XLA Modules:
  0.0 26.1 jit_solution(7598884117525642202)
XLA Ops:
  0.0 0.0 copy-start.1
  0.0 0.0 copy-start.4
  0.0 0.0 copy-start.3
  0.0 0.0 copy-start.2
  0.0 0.0 copy-start
  0.0 1.2 %pack.1 = (f32[28,512]{1,0:T(8,128)S(1)}, f32[28,512]{1,0:T(8,128)S(1)}, f32[2,7,8,512]{3,2,1,0:T(8,128)S(1)}, s32[8,512]{1,0:T(8,128)S(1)}) custom-call(f32[3,128,512]{2,1,0:T(8,128)} %state.1, s32[128,512]{1,0:T(8,128)} %cut.1, s32[128,512]{1,0:T(8,128)} %fraction.1, s32[128,512]{1,0:T(8,128)} %code.1, s32[1,4]{1,0:T(1,128)} %flags_in.1, f32[2,128,512]{2,1,0:T(8,128)} %offset.1), custom_call_target="tpu_custom_call" | custom-call | tf_op jit(solution)/shard_map/pack/pallas_call | solution.py:316
  1.3 0.9 %collective-permute-start = (f32[28,512]{1,0:T(8,128)S(1)}, f32[28,512]{1,0:T(8,128)S(1)}, u32[]{:S(2)}, u32[]{:S(2)}) collective-permute-start(f32[28,512]{1,0:T(8,128)S(1)} %get-tuple-element.19), channel_id=1, source_target_pairs={{0,32},{1,33},{2,34},{3,35},{4,36},{5,37},{6,38},{7,39},{8,40},{9,... | collective-permute-start | bytes 172040 | tf_op jit(solution)/shard_map/ppermute | solution.py:34
  2.2 2.9 %collective-permute-start.1 = (f32[28,512]{1,0:T(8,128)S(1)}, f32[28,512]{1,0:T(8,128)S(1)}, u32[]{:S(2)}, u32[]{:S(2)}) collective-permute-start(f32[28,512]{1,0:T(8,128)S(1)} %get-tuple-element.20), channel_id=1, source_target_pairs={{0,1},{1,0},{2,3},{3,2},{4,5},{5,4},{6,7},{7,6},{8,9},{9,8},{10,11... | collective-permute-start | bytes 172040 | tf_op jit(solution)/shard_map/ppermute | solution.py:34
  5.1 0.0 copy-done.1
  5.1 0.0 copy-done.4
  5.1 0.0 copy-done.3
  5.1 0.0 copy-done.2
  5.1 0.0 copy-done
  5.1 5.4 %first.1 = (f32[28,256]{1,0:T(8,128)S(1)}, f32[28,256]{1,0:T(8,128)S(1)}, f32[2,7,8,128]{3,2,1,0:T(8,128)S(1)}, f32[9,4,144,128]{3,2,1,0:T(8,128)S(1)}, f32[6,4,...) custom-call(f32[3,128,512]{2,1,0:T(8,128)S(1)} %copy-done, ...), custom_call_target="tpu_custom_call" | custom-call | flops 30000000 | bytes 1000000 | tf_op jit(solution)/shard_map/first/pallas_call | solution.py:442
  10.5 0.0 collective-permute-done.h0
  10.5 0.0 collective-permute-done.1.h1
  10.5 0.1 corner.1
  10.6 0.1 collective-permute-start.2
  10.7 6.7 %collective-permute-start.3 = (f32[28,256]{1,0:T(8,128)S(1)}, f32[28,256]{1,0:T(8,128)S(1)}, u32[]{:S(2)}, u32[]{:S(2)}) collective-permute-start(f32[28,256]{1,0:T(8,128)S(1)} %get-tuple-element.26), channel_id=1, source_target_pairs={{0,32},{1,2},{2,1},{3,4},{4,3},{5,6},{6,5},{7,8},{8,7},{9,10},{10,... | collective-permute-start | bytes 86024 | tf_op jit(solution)/shard_map/ppermute | solution.py:34
  17.5 5.5 %second.1.inner_out = f32[3,128,512]{2,1,0:T(8,128)S(1)} custom-call(f32[9,4,144,128]{3,2,1,0:T(8,128)S(1)} %get-tuple-element.28.mk, f32[6,4,144,128]{3,2,1,0:T(8,128)S(1)} %get-tuple-element.29.raw, f32[1,4,144,128]{3,2,1,0:T(8,128)S(1)} %get-tuple-element.30.rc, f32[4,4,144,128]{3,2,1,0:T(8,128)S(1)} %get-tuple-element.31.seen, ...), custom_call_target="tpu_custom_call" | custom-call | flops 30000000 | bytes 1000000 | tf_op jit(solution)/shard_map/second/pallas_call | solution.py:462
  22.9 0.0 collective-permute-done.2.c0
  22.9 0.0 collective-permute-done.3.c1
  23.0 3.1 %rim.1 = f32[3,128,512]{2,1,0:T(8,128)} custom-call(f32[28,512]{1,0:T(8,128)S(1)} %collective-permute-done.h0, f32[28,512]{1,0:T(8,128)S(1)} %collective-permute-done.1.h1, f32[28,256]{1,0:T(8,128)S(1)} %collective-permute-done.2.c0, f32[28,256]{1,0:T(8,128)S(1)} %collective-permute-done.3.c1, f32[2,7,8,512]{3,2,1,0:T(8,128)S(1)} %get-tuple-element.22.own_rows, ...), custom_call_target="tpu_custom_call" | custom-call | flops 10000000 | bytes 1000000 | tf_op jit(solution)/shard_map/rim/pallas_call | solution.py:591
Async XLA Ops:
  0.0 5.1 %copy-start.1 = (f32[2,128,512]{2,1,0:T(8,128)S(1)}, f32[2,128,512]{2,1,0:T(8,128)}, u32[]{:S(2)}) copy-start(f32[2,128,512]{2,1,0:T(8,128)} %offset.1) | copy-start | bytes 1572868
  0.0 5.1 %copy-start.4 = (s32[128,512]{1,0:T(8,128)S(1)}, s32[128,512]{1,0:T(8,128)}, u32[]{:S(2)}) copy-start(s32[128,512]{1,0:T(8,128)} %code.1) | copy-start | bytes 786436
  0.0 5.1 %copy-start.3 = (s32[128,512]{1,0:T(8,128)S(1)}, s32[128,512]{1,0:T(8,128)}, u32[]{:S(2)}) copy-start(s32[128,512]{1,0:T(8,128)} %fraction.1) | copy-start | bytes 786436
  0.0 5.1 %copy-start.2 = (s32[128,512]{1,0:T(8,128)S(1)}, s32[128,512]{1,0:T(8,128)}, u32[]{:S(2)}) copy-start(s32[128,512]{1,0:T(8,128)} %cut.1) | copy-start | bytes 786436
  0.0 5.1 %copy-start = (f32[3,128,512]{2,1,0:T(8,128)S(1)}, f32[3,128,512]{2,1,0:T(8,128)}, u32[]{:S(2)}) copy-start(f32[3,128,512]{2,1,0:T(8,128)} %state.1) | copy-start | bytes 2359300
  1.3 9.2 %collective-permute-start = (f32[28,512]{1,0:T(8,128)S(1)}, f32[28,512]{1,0:T(8,128)S(1)}, u32[]{:S(2)}, u32[]{:S(2)}) collective-permute-start(f32[28,512]{1,0:T(8,128)S(1)} %get-tuple-element.19), channel_id=1, source_target_pairs={{0,32},{1,33},{2,34},{3,35},{4,36},{5,37},{6,38},{7,39},{8,40},{9,... | collective-permute-start | bytes 172040 | tf_op jit(solution)/shard_map/ppermute | solution.py:34
  2.2 8.3 %collective-permute-start.1 = (f32[28,512]{1,0:T(8,128)S(1)}, f32[28,512]{1,0:T(8,128)S(1)}, u32[]{:S(2)}, u32[]{:S(2)}) collective-permute-start(f32[28,512]{1,0:T(8,128)S(1)} %get-tuple-element.20), channel_id=1, source_target_pairs={{0,1},{1,0},{2,3},{3,2},{4,5},{5,4},{6,7},{7,6},{8,9},{9,8},{10,11... | collective-permute-start | bytes 172040 | tf_op jit(solution)/shard_map/ppermute | solution.py:34
  10.6 12.3 %collective-permute-start.2 = (f32[28,256]{1,0:T(8,128)S(1)}, f32[28,256]{1,0:T(8,128)S(1)}, u32[]{:S(2)}, u32[]{:S(2)}) collective-permute-start(f32[28,256]{1,0:T(8,128)S(1)} %get-tuple-element.25), channel_id=1, source_target_pairs={{0,1},{1,0},{2,3},{3,2},{4,5},{5,4},{6,7},{7,6},{8,9},{9,8},{10,11... | collective-permute-start | bytes 86024 | tf_op jit(solution)/shard_map/ppermute | solution.py:34
  10.7 12.2 %collective-permute-start.3 = (f32[28,256]{1,0:T(8,128)S(1)}, f32[28,256]{1,0:T(8,128)S(1)}, u32[]{:S(2)}, u32[]{:S(2)}) collective-permute-start(f32[28,256]{1,0:T(8,128)S(1)} %get-tuple-element.26), channel_id=1, source_target_pairs={{0,32},{1,2},{2,1},{3,4},{4,3},{5,6},{6,5},{7,8},{8,7},{9,10},{10,... | collective-permute-start | bytes 86024 | tf_op jit(solution)/shard_map/ppermute | solution.py:34

commit v5 on v4

--- a/solution.py
+++ b/solution.py
@@ -347,12 +347,15 @@
     east = [(t + 1) % ntile for t in tiles]
 
     even_x = lax.rem(lax.axis_index("tx"), 2) == 0
-    for side, t in enumerate((0, ntile - 1)):
+    ends = []
+    for t in (0, ntile - 1):
         ls = pl.ds(t * LANES, LANES)
-        got = strip_fields(state, cut, fraction, code, offset, slice(None), ls, limit[0:1, ls])
-        first = 0 if side == 0 else LANES - 8
-        for f in range(FIELDS):
-            own_cols[side, f, :, :] = got[f].T[first : first + 8, :]
+        ends.append(strip_fields(state, cut, fraction, code, offset, slice(None), ls, limit[0:1, ls]))
+    half = lax.broadcasted_iota(jnp.int32, (rows, LANES), 1) < LANES // 2
+    for f in range(FIELDS):
+        turned = jnp.where(half, ends[0][f], ends[1][f]).T
+        own_cols[0, f, :, :] = turned[0:8, :]
+        own_cols[1, f, :, :] = turned[LANES - 8 :, :]
     for f in range(FIELDS):
         left = own_cols[0, f, 0:4, :]
         right = own_cols[1, f, 4:8, :]

time: 26.2 us -> 26.1 us (level)
  transfers between devices with their start and end apart: 4 -> 4, of which waited for: 0 -> 0; matrix products, arithmetic and copies ran while one was open for 0% -> 0% of each run, Pallas kernels for 42% -> 41%
where the time goes in v5:
time: 26.1 us; the launch traced here: 26 us
  Pallas kernels  15.2 us (58%)
  starting transfers between devices  10.6 us (41%)
    ppermute x4, starting transfers between devices, paired(): return lax.ppermute(value, ('ty', 'tx'), sorted(pairs))  10.6 us
    pallas_call x1, Pallas kernels, second_part(): pl.pallas_call(second_kernel, out_shape=pltpu.VMEM((3, rows, ntile * LANE...  5.45 us
    pallas_call x1, Pallas kernels, first_part(): pl.pallas_call(first_kernel, out_shape=(pltpu.VMEM((PACKED, 2 * LANES), f...  5.3 us
    pallas_call x1, Pallas kernels, rim(): pl.pallas_call(rim_kernel, out_shape=pltpu.HBM((3, rows, cols), f32), in_...  3.15 us
    pallas_call x1, Pallas kernels, pack(): pl.pallas_call(pack_kernel, out_shape=(pltpu.VMEM((PACKED, cols), f32), p...  1.24 us
  transfers between devices with their start and end apart: 4, of which 0 were waited for; matrix products, arithmetic and copies ran while one was open for 0% of the time, Pallas kernels for 41%

profile of v5, /device:TPU:14, one launch (start us, length us, event | category | flops | bytes accessed | tf_op | source)
XLA Modules:
  0.0 26.0 jit_solution(3044139150965705796)
XLA Ops:
  0.0 0.0 copy-start.1
  0.0 0.0 copy-start.4
  0.0 0.0 copy-start.3
  0.0 0.0 copy-start.2
  0.0 0.0 copy-start
  0.0 1.2 %pack.1 = (f32[28,512]{1,0:T(8,128)S(1)}, f32[28,512]{1,0:T(8,128)S(1)}, f32[2,7,8,512]{3,2,1,0:T(8,128)S(1)}, s32[8,512]{1,0:T(8,128)S(1)}) custom-call(f32[3,128,512]{2,1,0:T(8,128)} %state.1, s32[128,512]{1,0:T(8,128)} %cut.1, s32[128,512]{1,0:T(8,128)} %fraction.1, s32[128,512]{1,0:T(8,128)} %code.1, s32[1,4]{1,0:T(1,128)} %flags_in.1, f32[2,128,512]{2,1,0:T(8,128)} %offset.1), custom_call_target="tpu_custom_call" | custom-call | tf_op jit(solution)/shard_map/pack/pallas_call | solution.py:316
  1.3 0.9 %collective-permute-start = (f32[28,512]{1,0:T(8,128)S(1)}, f32[28,512]{1,0:T(8,128)S(1)}, u32[]{:S(2)}, u32[]{:S(2)}) collective-permute-start(f32[28,512]{1,0:T(8,128)S(1)} %get-tuple-element.19), channel_id=1, source_target_pairs={{0,32},{1,33},{2,34},{3,35},{4,36},{5,37},{6,38},{7,39},{8,40},{9,... | collective-permute-start | bytes 172040 | tf_op jit(solution)/shard_map/ppermute | solution.py:34
  2.2 2.9 %collective-permute-start.1 = (f32[28,512]{1,0:T(8,128)S(1)}, f32[28,512]{1,0:T(8,128)S(1)}, u32[]{:S(2)}, u32[]{:S(2)}) collective-permute-start(f32[28,512]{1,0:T(8,128)S(1)} %get-tuple-element.20), channel_id=1, source_target_pairs={{0,1},{1,0},{2,3},{3,2},{4,5},{5,4},{6,7},{7,6},{8,9},{9,8},{10,11... | collective-permute-start | bytes 172040 | tf_op jit(solution)/shard_map/ppermute | solution.py:34
  5.1 0.0 copy-done.1
  5.1 0.0 copy-done.4
  5.1 0.0 copy-done.3
  5.1 0.0 copy-done.2
  5.1 0.0 copy-done
  5.1 5.3 %first.1 = (f32[28,256]{1,0:T(8,128)S(1)}, f32[28,256]{1,0:T(8,128)S(1)}, f32[2,7,8,128]{3,2,1,0:T(8,128)S(1)}, f32[9,4,144,128]{3,2,1,0:T(8,128)S(1)}, f32[6,4,...) custom-call(f32[3,128,512]{2,1,0:T(8,128)S(1)} %copy-done, ...), custom_call_target="tpu_custom_call" | custom-call | flops 30000000 | bytes 1000000 | tf_op jit(solution)/shard_map/first/pallas_call | solution.py:445
  10.4 0.0 collective-permute-done.h0
  10.4 0.0 collective-permute-done.1.h1
  10.4 0.1 corner.1
  10.5 0.1 collective-permute-start.2
  10.6 6.7 %collective-permute-start.3 = (f32[28,256]{1,0:T(8,128)S(1)}, f32[28,256]{1,0:T(8,128)S(1)}, u32[]{:S(2)}, u32[]{:S(2)}) collective-permute-start(f32[28,256]{1,0:T(8,128)S(1)} %get-tuple-element.26), channel_id=1, source_target_pairs={{0,32},{1,2},{2,1},{3,4},{4,3},{5,6},{6,5},{7,8},{8,7},{9,10},{10,... | collective-permute-start | bytes 86024 | tf_op jit(solution)/shard_map/ppermute | solution.py:34
  17.4 5.5 %second.1.inner_out = f32[3,128,512]{2,1,0:T(8,128)S(1)} custom-call(f32[9,4,144,128]{3,2,1,0:T(8,128)S(1)} %get-tuple-element.28.mk, f32[6,4,144,128]{3,2,1,0:T(8,128)S(1)} %get-tuple-element.29.raw, f32[1,4,144,128]{3,2,1,0:T(8,128)S(1)} %get-tuple-element.30.rc, f32[4,4,144,128]{3,2,1,0:T(8,128)S(1)} %get-tuple-element.31.seen, ...), custom_call_target="tpu_custom_call" | custom-call | flops 30000000 | bytes 1000000 | tf_op jit(solution)/shard_map/second/pallas_call | solution.py:465
  22.8 0.0 collective-permute-done.2.c0
  22.8 0.0 collective-permute-done.3.c1
  22.8 3.1 %rim.1 = f32[3,128,512]{2,1,0:T(8,128)} custom-call(f32[28,512]{1,0:T(8,128)S(1)} %collective-permute-done.h0, f32[28,512]{1,0:T(8,128)S(1)} %collective-permute-done.1.h1, f32[28,256]{1,0:T(8,128)S(1)} %collective-permute-done.2.c0, f32[28,256]{1,0:T(8,128)S(1)} %collective-permute-done.3.c1, f32[2,7,8,512]{3,2,1,0:T(8,128)S(1)} %get-tuple-element.22.own_rows, ...), custom_call_target="tpu_custom_call" | custom-call | flops 10000000 | bytes 1000000 | tf_op jit(solution)/shard_map/rim/pallas_call | solution.py:594
Async XLA Ops:
  0.0 5.1 %copy-start.1 = (f32[2,128,512]{2,1,0:T(8,128)S(1)}, f32[2,128,512]{2,1,0:T(8,128)}, u32[]{:S(2)}) copy-start(f32[2,128,512]{2,1,0:T(8,128)} %offset.1) | copy-start | bytes 1572868
  0.0 5.1 %copy-start.4 = (s32[128,512]{1,0:T(8,128)S(1)}, s32[128,512]{1,0:T(8,128)}, u32[]{:S(2)}) copy-start(s32[128,512]{1,0:T(8,128)} %code.1) | copy-start | bytes 786436
  0.0 5.1 %copy-start.3 = (s32[128,512]{1,0:T(8,128)S(1)}, s32[128,512]{1,0:T(8,128)}, u32[]{:S(2)}) copy-start(s32[128,512]{1,0:T(8,128)} %fraction.1) | copy-start | bytes 786436
  0.0 5.1 %copy-start.2 = (s32[128,512]{1,0:T(8,128)S(1)}, s32[128,512]{1,0:T(8,128)}, u32[]{:S(2)}) copy-start(s32[128,512]{1,0:T(8,128)} %cut.1) | copy-start | bytes 786436
  0.0 5.1 %copy-start = (f32[3,128,512]{2,1,0:T(8,128)S(1)}, f32[3,128,512]{2,1,0:T(8,128)}, u32[]{:S(2)}) copy-start(f32[3,128,512]{2,1,0:T(8,128)} %state.1) | copy-start | bytes 2359300
  1.3 9.1 %collective-permute-start = (f32[28,512]{1,0:T(8,128)S(1)}, f32[28,512]{1,0:T(8,128)S(1)}, u32[]{:S(2)}, u32[]{:S(2)}) collective-permute-start(f32[28,512]{1,0:T(8,128)S(1)} %get-tuple-element.19), channel_id=1, source_target_pairs={{0,32},{1,33},{2,34},{3,35},{4,36},{5,37},{6,38},{7,39},{8,40},{9,... | collective-permute-start | bytes 172040 | tf_op jit(solution)/shard_map/ppermute | solution.py:34
  2.2 8.2 %collective-permute-start.1 = (f32[28,512]{1,0:T(8,128)S(1)}, f32[28,512]{1,0:T(8,128)S(1)}, u32[]{:S(2)}, u32[]{:S(2)}) collective-permute-start(f32[28,512]{1,0:T(8,128)S(1)} %get-tuple-element.20), channel_id=1, source_target_pairs={{0,1},{1,0},{2,3},{3,2},{4,5},{5,4},{6,7},{7,6},{8,9},{9,8},{10,11... | collective-permute-start | bytes 172040 | tf_op jit(solution)/shard_map/ppermute | solution.py:34
  10.5 12.3 %collective-permute-start.2 = (f32[28,256]{1,0:T(8,128)S(1)}, f32[28,256]{1,0:T(8,128)S(1)}, u32[]{:S(2)}, u32[]{:S(2)}) collective-permute-start(f32[28,256]{1,0:T(8,128)S(1)} %get-tuple-element.25), channel_id=1, source_target_pairs={{0,1},{1,0},{2,3},{3,2},{4,5},{5,4},{6,7},{7,6},{8,9},{9,8},{10,11... | collective-permute-start | bytes 86024 | tf_op jit(solution)/shard_map/ppermute | solution.py:34
  10.6 12.2 %collective-permute-start.3 = (f32[28,256]{1,0:T(8,128)S(1)}, f32[28,256]{1,0:T(8,128)S(1)}, u32[]{:S(2)}, u32[]{:S(2)}) collective-permute-start(f32[28,256]{1,0:T(8,128)S(1)} %get-tuple-element.26), channel_id=1, source_target_pairs={{0,32},{1,2},{2,1},{3,4},{4,3},{5,6},{6,5},{7,8},{8,7},{9,10},{10,... | collective-permute-start | bytes 86024 | tf_op jit(solution)/shard_map/ppermute | solution.py:34
